TPU v7x, 32 devices: a whole 2x2x4 slice. The times are simulated.
32 devices in a mesh: grp: 2 (over x), panel: 16 (over z, y, core).
Axes of the slice: x: 2, y: 2, z: 4, core: 2. Of those that a mesh axis runs over, the one named last changes fastest.
Arguments:
- density: bfloat16 [1024, 16, 128], P(('grp', 'panel')), parts along dimension 0, may hold values from -6 to 6
- near_blocks: bfloat16 [1024, 8, 128, 128], P(('grp', 'panel')), parts along dimension 0, may hold values from -0.1875 to 0.1875
- neighbours: int32 [1024, 8], P(('grp', 'panel')), parts along dimension 0, may hold values from 0 to 511, as said below
- counts: int32 [1024], P(('grp', 'panel')), parts along dimension 0, may hold values from 1 to 8, as said below
- coarse_map: int32 [1024], P(('grp', 'panel')), parts along dimension 0, may hold values from 0 to 31, as said below
- restrict: bfloat16 [1024, 128, 128], P(('grp', 'panel')), parts along dimension 0, may hold values from -0.125 to 0.125
- evaluate: bfloat16 [1024, 128, 128], P(('grp', 'panel')), parts along dimension 0, may hold values from -0.5 to 0.5
- coupling: float32 [64, 32], P(('grp', 'panel')), parts along dimension 0, as said below
Outputs:
- potential: bfloat16 [1024, 16, 128], P(('grp', 'panel')), parts along dimension 0
There are 2 independent parts, one for each index of `grp`. A program takes and returns all parts, laid end to end along the dimension named above; each array names one. Nothing has to cross between parts.
Inputs may be any that keep to these rules, and one draw needn't show every extreme that they name: `neighbours`: slot 0 of block b is b itself; every entry lies within 16 blocks of b; in every draw some entry lies exactly 16 blocks below its block and some exactly 16 above. `counts`: every device holds blocks with all 8 slots live. `coarse_map`: block b's coarse cluster is one of the 2 clusters from (b // 32) * 2 on. `coupling`: the matrix is symmetric.
All inputs are finite; a program needn't handle non-finite values.
Results may differ from a plain program's by a relative error of at most 0.0042.
Values may be sent and summed in bfloat16 or wider, within the bound.
No kernel may reach another device: no remote copies, remote signals or barrier semaphores. Data moves between devices by JAX's collectives and lax.ppermute only.
A program may use at most 64 MiB of HBM per device.

v0:
```python
import jax
import jax.numpy as jnp
from jax import lax
from jax.sharding import PartitionSpec as P


def extended_2(block, sides, width):
    for axis, dim in sides:
        count = lax.axis_size(axis)
        forward = [(i, i + 1) for i in range(count - 1)]
        backward = [(target, source) for source, target in forward]
        low = lax.ppermute(
            lax.slice_in_dim(block, block.shape[dim] - width, None, axis=dim), axis, forward
        )
        high = lax.ppermute(lax.slice_in_dim(block, 0, width, axis=dim), axis, backward)
        block = jnp.concatenate([low, block, high], axis=dim)
    return block


def shards(density, near_blocks, neighbours, counts, coarse_map, restrict, evaluate, coupling):
    blk_count, columns, panels = density.shape
    reach_blocks = blk_count // 2
    anchor = lax.axis_index("panel") * blk_count
    extended = extended_2(density, (("panel", 0),), reach_blocks)
    local_ids = neighbours - (anchor - reach_blocks)
    picked = jnp.take(extended, local_ids, axis=0)
    slot_ids = jnp.arange(neighbours.shape[1])
    live_slots = slot_ids[None, :] < counts[:, None]
    picked = jnp.where(live_slots[:, :, None, None], picked, jnp.zeros((), jnp.bfloat16))
    near_part = jnp.einsum(
        "bjpq,bjrq->brp", near_blocks, picked, preferred_element_type=jnp.float32
    )
    coarse_dev = coupling.shape[0]
    expand_terms = restrict.shape[1]
    block_terms = jnp.einsum("bkp,brp->brk", restrict, density, preferred_element_type=jnp.float32)
    block_terms = block_terms.reshape(blk_count, columns * expand_terms)
    own_ids = coarse_map - lax.axis_index("panel") * coarse_dev
    onehot = (own_ids[None, :] == jnp.arange(coarse_dev)[:, None]).astype(jnp.float32)
    moments = jnp.dot(onehot, block_terms, precision=lax.Precision.HIGHEST)
    all_moments = lax.all_gather(moments, "panel", axis=0, tiled=True)
    local_full = jnp.dot(coupling, all_moments, precision=lax.Precision.HIGHEST)
    local_exp = local_full.astype(jnp.bfloat16)
    spread = jnp.dot(onehot.T.astype(jnp.bfloat16), local_exp, preferred_element_type=jnp.float32)
    spread = spread.astype(jnp.bfloat16).reshape(blk_count, columns, expand_terms)
    far_part = jnp.einsum("bkp,brk->brp", evaluate, spread, preferred_element_type=jnp.float32)
    return (near_part + far_part).astype(jnp.bfloat16)


def solution(mesh):
    placed = (
        P(("grp", "panel"), None, None),
        P(("grp", "panel"), None, None, None),
        P(("grp", "panel"), None),
        P(("grp", "panel")),
        P(("grp", "panel")),
        P(("grp", "panel"), None, None),
        P(("grp", "panel"), None, None),
        P(("grp", "panel"), None),
    )
    return jax.shard_map(
        shards,
        mesh=mesh,
        in_specs=placed,
        out_specs=P(("grp", "panel"), None, None),
        check_vma=False,
    )
```

profile of v0, /device:TPU:0, one launch (start us, length us, event | category | flops | bytes accessed | tf_op | source)
XLA Modules:
  0.0 43.6 jit_solution(7117227602017321483)
XLA Ops:
  0.0 0.0 copy-start
  0.0 0.0 copy-start.1
  0.0 1.0 %fusion.16 = (bf16[16,16,128]{2,1,0:T(8,128)(2,1)S(1)}, bf16[16,16,128]{2,1,0:T(8,128)(2,1)S(1)}) fusion(bf16[32,16,128]{2,1,0:T(8,128)(2,1)} %param.8), kind=kLoop, calls=%fused_computation.30 | loop fusion | bytes 262144 | tf_op jit(solution)/shard_map/slice | solution.py:13
  1.0 2.4 %collective-permute-start = (bf16[16,16,128]{2,1,0:T(8,128)(2,1)S(1)}, bf16[16,16,128]{2,1,0:T(8,128)(2,1)S(1)}, u32[]{:S(2)}, u32[]{:S(2)}) collective-permute-start(bf16[16,16,128]{2,1,0:T(8,128)(2,1)S(1)} %get-tuple-element.7), channel_id=1, source_target_pairs={{0,1},{1,2},{2,3},{3,4},{4,5},{5,6},{6,7},{7,8},{8,9},{9,10},{10,1... | collective-permute-start | bytes 196616 | tf_op jit(solution)/shard_map/ppermute | solution.py:12
  3.4 1.3 %collective-permute-start.1 = (bf16[16,16,128]{2,1,0:T(8,128)(2,1)S(1)}, bf16[16,16,128]{2,1,0:T(8,128)(2,1)S(1)}, u32[]{:S(2)}, u32[]{:S(2)}) collective-permute-start(bf16[16,16,128]{2,1,0:T(8,128)(2,1)S(1)} %get-tuple-element.8), channel_id=1, source_target_pairs={{1,0},{2,1},{3,2},{4,3},{5,4},{6,5},{7,6},{8,7},{9,8},{10,9},{11,1... | collective-permute-start | bytes 196616 | tf_op jit(solution)/shard_map/ppermute | solution.py:15
  4.8 0.7 %compare_and_fusion = (pred[32,8]{0,1:T(8,128)(4,1)S(1)}, s32[32,8]{0,1:T(8,128)S(1)}) fusion(s32[32,8]{0,1:T(8,128)} %param.10, s32[]{:T(128)S(6)} %sub.15), kind=kLoop, calls=%fused_computation.23 | loop fusion | flops 1792 | bytes 2308 | tf_op jit(solution)/shard_map/jit(_take)/and | solution.py:26
  5.4 0.1 copy.13
  5.5 0.1 reshape.37
  5.6 0.1 copy.12
  5.7 0.7 %iota_compare_fusion.1 = pred[32,8]{1,0:T(8,128)(4,1)S(1)} fusion(s32[32]{0:T(128)} %param.11), kind=kLoop, calls=%fused_computation.19 | loop fusion | flops 256 | bytes 384 | tf_op jit(solution)/shard_map/lt | solution.py:28
  6.4 0.0 copy-done
  6.4 1.5 %fusion.17 = f32[32,16,128]{2,1,0:T(8,128)S(1)} fusion(bf16[32,16,128]{2,1,0:T(8,128)(2,1)} %param.8, bf16[32,128,128]{2,1,0:T(8,128)(2,1)S(1)} %copy-done), kind=kOutput, calls=%fused_computation.31 | convolution fusion | flops 16777216 | bytes 1441792 | tf_op jit(solution)/shard_map/bkp,brp->brk/dot_general | solution.py:35
  8.0 0.7 %broadcast_subtract_fusion = s32[32]{0:T(128)S(1)} fusion(s32[32]{0:T(128)} %param.12, s32[]{:T(128)S(6)} %mul.7), kind=kLoop, calls=%fused_computation.27 | loop fusion | flops 32 | bytes 260 | tf_op jit(solution)/shard_map/sub | solution.py:37
  8.7 0.3 convolution_bitcast_fusion
  8.9 25.7 %all-gather = f32[16,2,2048]{2,1,0:T(2,128)S(1)} all-gather(f32[1,2,2048]{2,1,0:T(2,128)S(1)} %convolution_bitcast_fusion), channel_id=1, replica_groups=mesh['grp'=2,'panel'=16] {'panel'}, dimensions={0}, use_global_device_ids=true | all-gather | bytes 278528 | tf_op jit(solution)/shard_map/all_gather | solution.py:40
  34.6 0.2 reshape.46
  34.8 0.9 %convolution_convert_fusion.1 = bf16[2048,2]{0,1:T(2,128)(2,1)S(1)} fusion(f32[32,2048]{1,0:T(8,128)S(1)} %reshape.46, f32[2,32]{1,0:T(2,128)} %param.15), kind=kOutput, calls=%fused_computation.3 | convolution fusion | flops 1576960 | bytes 270592 | tf_op jit(solution)/shard_map/dot_general | solution.py:41
  35.8 0.2 fusion.1
  36.0 0.0 collective-permute-done
  36.1 0.0 collective-permute-done.1
  36.1 0.9 %pad_maximum_fusion = bf16[64,16,128]{2,1,0:T(8,128)(2,1)S(1)} fusion(bf16[16,16,128]{2,1,0:T(8,128)(2,1)S(1)} %collective-permute-done.1, bf16[32,16,128]{2,1,0:T(8,128)(2,1)} %param.8, bf16[16,16,128]{2,1,0:T(8,128)(2,1)S(1)} %collective-permute-done), kind=kLoop, calls=%fused_computation.16 | loop fusion | flops 262144 | bytes 524288 | tf_op jit(solution)/shard_map/concatenate | solution.py:16
  37.0 0.8 %gather_fusion = bf16[256,16,128]{2,1,0:T(8,128)(2,1)S(1)} fusion(bf16[64,16,128]{2,1,0:T(8,128)(2,1)S(1)} %pad_maximum_fusion, s32[1024]{0:T(1024)S(1)} %pad_clamp_fusion), kind=kCustom, calls=%fused_computation | custom fusion | bytes 2098176 | tf_op jit(solution)/shard_map/jit(_take)/gather | solution.py:26
  37.9 4.7 %convolution_bitcast_fusion.1 = f32[32,16,128]{2,1,0:T(8,128)S(1)} fusion(bf16[32,8,128,128]{3,2,1,0:T(8,128)(2,1)} %param.9, bf16[32,8,16,128]{3,2,1,0:T(8,128)(2,1)S(1)} %bitcast.21, pred[32,8]{1,0:T(8,128)(4,1)S(1)} %copy.12, pred[32,8]{1,0:T(8,128)(4,1)S(1)} %iota_compare_fusion.1), kind=kOutput, calls=%fused_computation.5 | convolution fusion | flops 135266304 | bytes 9699840 | tf_op jit(solution)/shard_map/bjpq,bjrq->brp/dot_general | solution.py:30
  42.6 0.0 copy-done.1
  42.6 1.1 %fusion = bf16[32,16,128]{2,1,0:T(8,128)(2,1)} fusion(f32[32,16,128]{2,1,0:T(8,128)S(1)} %convolution_bitcast_fusion.1, bf16[32,16,128]{2,1,0:T(8,128)(2,1)S(1)} %bitcast.23, bf16[32,128,128]{2,1,0:T(8,128)(2,1)S(1)} %copy-done.1), kind=kOutput, calls=%fused_computation.6 | convolution fusion | flops 16908288 | bytes 1572864 | tf_op jit(solution)/shard_map/bkp,brk->brp/dot_general | solution.py:45
  (2 shorter events, 0.0 us)
Async XLA Ops:
  0.0 6.4 %copy-start = (bf16[32,128,128]{2,1,0:T(8,128)(2,1)S(1)}, bf16[32,128,128]{2,1,0:T(8,128)(2,1)}, u32[]{:S(2)}) copy-start(bf16[32,128,128]{2,1,0:T(8,128)(2,1)} %param.13) | copy-start | bytes 3145732
  0.0 42.6 %copy-start.1 = (bf16[32,128,128]{2,1,0:T(8,128)(2,1)S(1)}, bf16[32,128,128]{2,1,0:T(8,128)(2,1)}, u32[]{:S(2)}) copy-start(bf16[32,128,128]{2,1,0:T(8,128)(2,1)} %param.14) | copy-start | bytes 3145732
  1.0 35.0 %collective-permute-start = (bf16[16,16,128]{2,1,0:T(8,128)(2,1)S(1)}, bf16[16,16,128]{2,1,0:T(8,128)(2,1)S(1)}, u32[]{:S(2)}, u32[]{:S(2)}) collective-permute-start(bf16[16,16,128]{2,1,0:T(8,128)(2,1)S(1)} %get-tuple-element.7), channel_id=1, source_target_pairs={{0,1},{1,2},{2,3},{3,4},{4,5},{5,6},{6,7},{7,8},{8,9},{9,10},{10,1... | collective-permute-start | bytes 196616 | tf_op jit(solution)/shard_map/ppermute | solution.py:12
  3.4 32.6 %collective-permute-start.1 = (bf16[16,16,128]{2,1,0:T(8,128)(2,1)S(1)}, bf16[16,16,128]{2,1,0:T(8,128)(2,1)S(1)}, u32[]{:S(2)}, u32[]{:S(2)}) collective-permute-start(bf16[16,16,128]{2,1,0:T(8,128)(2,1)S(1)} %get-tuple-element.8), channel_id=1, source_target_pairs={{1,0},{2,1},{3,2},{4,3},{5,4},{6,5},{7,6},{8,7},{9,8},{10,9},{11,1... | collective-permute-start | bytes 196616 | tf_op jit(solution)/shard_map/ppermute | solution.py:15
where the time goes:
time: 43.9 us; the launch traced here: 43.6 us
  blocking collectives  25.7 us (59%)
  matrix products  8.74 us (20%)
  starting transfers between devices  3.69 us (8%)
  other arithmetic  3.06 us (7%)
  local copies, waits for them, and re-layouts  2.34 us (5%)
    all_gather x1, blocking collectives, shards(): all_moments = lax.all_gather(moments, 'panel', axis=0, tiled=True)  25.7 us
    dot_general x1, matrix products, shards(): jnp.einsum('bjpq,bjrq->brp', near_blocks, picked, preferred_element_type=...  4.7 us
    ppermute x1, starting transfers between devices, extended_2(): lax.ppermute(lax.slice_in_dim(block, block.shape[dim] - width, None, axis...  2.4 us
    dot_general x1, matrix products, shards(): jnp.einsum('bkp,brp->brk', restrict, density, preferred_element_type=jnp....  1.53 us
    ppermute x1, starting transfers between devices, extended_2(): lax.ppermute(lax.slice_in_dim(block, 0, width, axis=dim), axis, backward)  1.29 us
    dot_general x1, matrix products, shards(): jnp.einsum('bkp,brk->brp', evaluate, spread, preferred_element_type=jnp.f...  1.07 us
    slice x1, local copies, waits for them, and re-layouts, extended_2(): lax.slice_in_dim(block, block.shape[dim] - width, None, axis=dim)  1.03 us
    dot_general x1, matrix products, shards(): local_full = jnp.dot(coupling, all_moments, precision=lax.Precision.HIGHEST)  0.94 us
  transfers between devices with their start and end apart: 2, of which 0 were waited for; matrix products, arithmetic and copies ran while one was open for 13% of the time, Pallas kernels for 0%

commit v1 on v0

v1 whole, which is shorter than its diff:
```python
import functools

import jax
import jax.numpy as jnp
from jax import lax
from jax.experimental import pallas as pl
from jax.experimental.pallas import tpu as pltpu
from jax.sharding import PartitionSpec as P

F32 = jnp.float32
BF16 = jnp.bfloat16
VMEM = pl.BlockSpec(memory_space=pltpu.VMEM)
HBM = pl.BlockSpec(memory_space=pltpu.HBM)
SMEM = pl.BlockSpec(memory_space=pltpu.SMEM)
NT = (((1,), (1,)), ((), ()))
NN = (((1,), (0,)), ((), ()))


def moments_kernel(chunks, coarse_in, density_in, restrict_in, out, kept, to_chip, to_off, coarse, restrict, sems):
    blk_count, columns, _ = density_in.shape
    groups = out.shape[0] // columns
    half = to_chip.shape[0]
    size = blk_count // chunks
    position = lax.axis_index("panel")
    odd = lax.rem(position, 2)
    first = position * groups
    copies = [
        pltpu.make_async_copy(density_in, kept, sems.at[0]),
        pltpu.make_async_copy(coarse_in, coarse, sems.at[1]),
    ]
    for i in range(chunks):
        part = pl.ds(i * size, size)
        copies.append(pltpu.make_async_copy(restrict_in.at[part], restrict.at[part], sems.at[2 + i]))
    for copy in copies:
        copy.start()
    copies[0].wait()
    to_chip[...] = kept[pl.ds((1 - odd) * half, half)]
    to_off[...] = kept[pl.ds(odd * half, half)]
    copies[1].wait()
    total = jnp.zeros(out.shape, F32)
    for b in range(0, blk_count, 2):
        if b % size == 0:
            copies[2 + b // size].wait()
        rows = []
        for c in range(groups):
            pair = []
            for i in (b, b + 1):
                here = (coarse[i] - first) == c
                block = kept[i]
                pair.append(jnp.where(here, block, jnp.zeros_like(block)))
            rows.append(jnp.concatenate(pair, axis=1))
        left = jnp.concatenate(rows, axis=0)
        right = jnp.concatenate([restrict[b], restrict[b + 1]], axis=1)
        total += lax.dot_general(left, right, NT, preferred_element_type=F32)
    out[...] = total.astype(out.dtype)


def near_kernel(begin, ids, counts, density, chip_halo, near_halo, far_halo, blocks, out, extended):
    blk_count, columns, panels = density.shape
    half = chip_halo.shape[0]
    slots = ids.shape[0]
    position = lax.axis_index("panel")
    odd = lax.rem(position, 2)
    quarter = lax.rem(position, 4)
    middle = jnp.logical_or(quarter == 1, quarter == 2)
    off_chip = jnp.where(middle, near_halo[...], far_halo[...])
    on_chip = chip_halo[...]
    extended[pl.ds(0, half)] = jnp.where(odd == 1, on_chip, off_chip)
    extended[pl.ds(half, blk_count)] = density[...]
    extended[pl.ds(half + blk_count, half)] = jnp.where(odd == 1, off_chip, on_chip)
    empty = blk_count + 2 * half
    extended[empty] = jnp.zeros((columns, panels), extended.dtype)
    shift = position * blk_count - half
    for at in range(out.shape[0]):
        b = begin + at
        live = counts[b]
        total = None
        for j in range(0, slots, 2):
            pair = []
            for i in (j, j + 1):
                slab = jnp.where(i < live, ids[i, b] - shift, empty)
                pair.append(extended[slab])
            left = jnp.concatenate(pair, axis=1)
            right = jnp.concatenate([blocks[b, j], blocks[b, j + 1]], axis=1)
            part = lax.dot_general(left, right, NT, preferred_element_type=F32)
            total = part if total is None else total + part
        out[at] = total


def weights_kernel(masks, coarse, coupling, weights, second):
    groups = coupling.shape[0]
    position = lax.axis_index("panel")
    first = position * groups
    tile = weights.shape[2:]
    for c in range(groups):
        for s, mask in enumerate(masks):
            source = lax.bitwise_xor(position, mask) * groups
            for g in range(groups):
                weights[c, s * groups + g] = jnp.full(tile, coupling[c, source + g], F32)
    for b in range(second.shape[0]):
        second[b] = jnp.full(tile, coarse[b] - first, jnp.int32)


def far_kernel(parts, weights, second, evaluate, *rest):
    moments, near, out = rest[:parts], rest[parts:-1], rest[-1]
    _, columns, panels = out.shape
    groups, _ = weights.shape[:2]
    local = []
    for c in range(groups):
        total = jnp.zeros((columns, panels), F32)
        s = 0
        for piece in moments:
            for at in range(0, piece.shape[0], columns):
                row = piece[pl.ds(at, columns)].astype(F32)
                weight = weights[c, s]
                total += row * jnp.concatenate([weight] * (columns // weight.shape[0]), axis=0)
                s += 1
        local.append(total.astype(BF16))
    left = jnp.concatenate(local, axis=0)
    begin = 0
    for part in near:
        for at in range(part.shape[0]):
            b = begin + at
            both = lax.dot_general(left, evaluate[b], NN, preferred_element_type=F32)
            pick = jnp.concatenate([second[b]] * (columns // second.shape[1]), axis=0)
            far = both[:columns]
            for c in range(1, groups):
                far = jnp.where(pick == c, both[c * columns : (c + 1) * columns], far)
            out[b] = (part[at] + far).astype(out.dtype)
        begin += part.shape[0]


def on_chip(*arrays):
    return [pltpu.with_memory_space_constraint(x, pltpu.VMEM) for x in arrays]


def in_hbm(*arrays):
    return [pltpu.with_memory_space_constraint(x, pltpu.HBM) for x in arrays]


def room(mebibytes):
    return pltpu.CompilerParams(vmem_limit_bytes=mebibytes << 20)


def cost(flops, moved):
    return pl.CostEstimate(flops=flops, bytes_accessed=moved, transcendentals=0)


def exchange(x, step):
    count = lax.axis_size("panel")
    return lax.ppermute(x, "panel", [(i, i ^ step) for i in range(count)])


def far_pairs(count):
    goes = {}
    for i in range(3, count - 1, 4):
        goes[i], goes[i + 1] = i + 1, i
    for i in range(5, count - 4, 4):
        goes[i], goes[i + 1] = i + 1, i
    for base in (0, count - 3):
        for i in range(3):
            goes[base + i] = base + (i + 1) % 3
    return sorted(goes.items())


def body(density, near_blocks, neighbours, counts, coarse_map, restrict, evaluate, coupling):
    blk_count, columns, panels = density.shape
    terms = restrict.shape[1]
    groups = coupling.shape[0]
    half = blk_count // 2
    count = lax.axis_size("panel")
    position = lax.axis_index("panel")
    odd = lax.rem(position, 2)

    steps = [(1 << bit) | 1 for bit in range(1, count.bit_length() - 1)] + [1]
    masks = [0]
    for step in steps:
        masks = masks + [mask ^ step for mask in masks]

    half_shape = (half, columns, panels)
    chunks = 4
    moments, kept, to_chip, to_off = pl.pallas_call(
        functools.partial(moments_kernel, chunks),
        out_shape=(
            pltpu.VMEM((groups * columns, terms), BF16),
            pltpu.VMEM(density.shape, BF16),
            pltpu.VMEM(half_shape, BF16),
            pltpu.VMEM(half_shape, BF16),
        ),
        in_specs=[HBM] * 3,
        out_specs=(VMEM,) * 4,
        scratch_shapes=[
            pltpu.SMEM(coarse_map.shape, jnp.int32),
            pltpu.VMEM(restrict.shape, BF16),
            pltpu.SemaphoreType.DMA((2 + chunks,)),
        ],
        compiler_params=room(8),
        cost_estimate=cost(10**10, 10**6),
        name="moments",
    )(*in_hbm(coarse_map, density, restrict))

    pieces = [moments]
    for at, step in enumerate(steps):
        sent = pieces[0] if at == 0 else jnp.concatenate(pieces, axis=0)
        pieces.append(exchange(sent, step))

    chip_halo = exchange(to_chip, 1)
    near_halo = exchange(to_off, 3)
    to_far = to_off
    far_halo = lax.ppermute(to_far, "panel", far_pairs(count))

    make_weights = pl.pallas_call(
        functools.partial(weights_kernel, masks),
        out_shape=(
            pltpu.VMEM((groups, groups * count, 8, 128), F32),
            pltpu.VMEM((blk_count, 8, 128), jnp.int32),
        ),
        in_specs=[SMEM, SMEM],
        out_specs=(VMEM, VMEM),
        compiler_params=room(4),
        cost_estimate=cost(10**11, 10**6),
        name="weights",
    )
    weights, second = make_weights(coarse_map, coupling)

    ids = neighbours.T
    near = []
    cuts = (0, 2 * blk_count // 3, blk_count)
    for begin, end in zip(cuts[:-1], cuts[1:]):
        call = (
            pl.pallas_call(
                functools.partial(near_kernel, begin),
                out_shape=pltpu.VMEM((end - begin, columns, panels), F32),
                in_specs=[SMEM, SMEM] + [VMEM] * 5,
                out_specs=VMEM,
                scratch_shapes=[pltpu.VMEM((blk_count + 2 * half + 1, columns, panels), BF16)],
                compiler_params=room(4),
                cost_estimate=cost(2 * 10**9, 10**6),
            )
        )
        near.append(call(ids, counts, *on_chip(kept, chip_halo, near_halo, far_halo, near_blocks)))

    return pl.pallas_call(
        functools.partial(far_kernel, len(pieces)),
        out_shape=jax.ShapeDtypeStruct(density.shape, BF16),
        in_specs=[VMEM] * (3 + len(pieces) + len(near)),
        out_specs=VMEM,
        compiler_params=room(4),
        cost_estimate=cost(10**9, 10**6),
        name="far",
    )(*on_chip(weights, second, evaluate, *pieces, *near))


def solution(mesh):
    placed = (
        P(("grp", "panel"), None, None),
        P(("grp", "panel"), None, None, None),
        P(("grp", "panel"), None),
        P(("grp", "panel")),
        P(("grp", "panel")),
        P(("grp", "panel"), None, None),
        P(("grp", "panel"), None, None),
        P(("grp", "panel"), None),
    )
    return jax.shard_map(
        body,
        mesh=mesh,
        in_specs=placed,
        out_specs=P(("grp", "panel"), None, None),
        check_vma=False,
    )
```

time: 43.9 us -> 19.6 us (0.45)
  blocking collectives: 25.7 us -> 0 us
  matrix products: 8.74 us -> 0 us
  Pallas kernels: 0 us -> 7.32 us
  starting transfers between devices: 3.69 us -> 9.08 us
  other arithmetic: 3.06 us -> 0.01 us
  waiting for transfers between devices: 0.01 us -> 2.84 us
  local copies, waits for them, and re-layouts: 2.34 us -> 0.04 us
    all_gather x1 -> x0, blocking collectives: 25.7 us -> none  [shards(): all_moments = lax.all_gather(moments, 'panel', axis=0, tiled=True)]
    dot_general x6 -> x0, matrix products: 8.74 us -> none  [the longest x1 4.7 us: shards(): jnp.einsum('bjpq,bjrq->brp', near_blocks, picked, preferred_element_type=...]
    pallas_call x0 -> x5, Pallas kernels: none -> 7.32 us  [the longest x2 3.66 us: body(): call(ids, counts, *on_chip(kept, chip_halo, near_halo, far_halo, near_blo...]
    ppermute x2 -> x7, starting transfers between devices: 3.69 us -> 9.08 us  [the longest x6 8.69 us: exchange(): return lax.ppermute(x, 'panel', [(i, i ^ step) for i in range(count)])]
    ppermute x2 -> x7, waiting for transfers between devices: 0.01 us -> 2.84 us  [the longest x6 2.84 us: exchange(): return lax.ppermute(x, 'panel', [(i, i ^ step) for i in range(count)])]
    slice x1 -> x0, local copies, waits for them, and re-layouts: 1.03 us -> none  [extended_2(): lax.slice_in_dim(block, block.shape[dim] - width, None, axis=dim)]
    concatenate x1 -> x3, other arithmetic: 0.94 us -> 0.01 us  [body(): sent = pieces[0] if at == 0 else jnp.concatenate(pieces, axis=0)]
    gather x1 -> x0, local copies, waits for them, and re-layouts: 0.85 us -> none  [shards(): picked = jnp.take(extended, local_ids, axis=0)]
  transfers between devices with their start and end apart: 2 -> 7, of which waited for: 0 -> 2; matrix products, arithmetic and copies ran while one was open for 13% -> 0% of each run, Pallas kernels for 0% -> 22%
where the time goes in v1:
time: 19.6 us; the launch traced here: 19.4 us
  starting transfers between devices  9.08 us (46%)
  Pallas kernels  7.32 us (37%)
  waiting for transfers between devices  2.84 us (14%)
    ppermute x6, starting transfers between devices, exchange(): return lax.ppermute(x, 'panel', [(i, i ^ step) for i in range(count)])  8.69 us
    pallas_call x2, Pallas kernels, body(): call(ids, counts, *on_chip(kept, chip_halo, near_halo, far_halo, near_blo...  3.66 us
    ppermute x6, waiting for transfers between devices, exchange(): return lax.ppermute(x, 'panel', [(i, i ^ step) for i in range(count)])  2.84 us
    pallas_call x1, Pallas kernels, body(): pl.pallas_call(functools.partial(moments_kernel, chunks), out_shape=(pltp...  1.89 us
    pallas_call x1, Pallas kernels, body(): pl.pallas_call(functools.partial(far_kernel, len(pieces)), out_shape=jax....  1.11 us
    pallas_call x1, Pallas kernels, body(): weights, second = make_weights(coarse_map, coupling)  0.66 us
    ppermute x1, starting transfers between devices, body(): far_halo = lax.ppermute(to_far, 'panel', far_pairs(count))  0.4 us
  transfers between devices with their start and end apart: 7, of which 2 were waited for; matrix products, arithmetic and copies ran while one was open for 0% of the time, Pallas kernels for 22%

profile of v1, /device:TPU:0, one launch (start us, length us, event | category | flops | bytes accessed | tf_op | source)
XLA Modules:
  0.0 19.4 jit_solution(4873958901158405684)
XLA Ops:
  0.0 0.0 copy-start.4
  0.0 0.0 copy-start.3
  0.0 1.9 %moments.1 = (bf16[32,128]{1,0:T(8,128)(2,1)S(1)}, bf16[32,16,128]{2,1,0:T(8,128)(2,1)S(1)}, bf16[16,16,128]{2,1,0:T(8,128)(2,1)S(1)}, bf16[16,16,128]{2,1,0:T(8,128)(2,1)S(1)}) custom-call(s32[32]{0:T(128)} %coarse_in.1, bf16[32,16,128]{2,1,0:T(8,128)(2,1)} %density_in.1, bf16[32,128,128]{2,1,0:T(8,128)(2,1)} %restrict_in.1), custom_call_target="tpu_custom_call" | custom-call | flops 10000000000 | bytes 1000000 | tf_op jit(solution)/shard_map/moments/pallas_call | solution.py:182
  1.9 2.5 %collective-permute-start = (bf16[32,128]{1,0:T(8,128)(2,1)S(1)}, bf16[32,128]{1,0:T(8,128)(2,1)S(1)}, u32[]{:S(2)}, u32[]{:S(2)}) collective-permute-start(bf16[32,128]{1,0:T(8,128)(2,1)S(1)} %get-tuple-element.13.rest_0_), channel_id=1, source_target_pairs={{0,3},{1,2},{2,1},{3,0},{4,7},{5,6},{6,5},{7,4},{8,11},{9,10},{10,... | collective-permute-start | bytes 24584 | tf_op jit(solution)/shard_map/ppermute | solution.py:151
  4.4 1.4 %collective-permute-done.rest_1_ = bf16[32,128]{1,0:T(8,128)(2,1)S(1)} collective-permute-done((bf16[32,128]{1,0:T(8,128)(2,1)S(1)}, bf16[32,128]{1,0:T(8,128)(2,1)S(1)}, u32[]{:S(2)}, u32[]{:S(2)}) %collective-permute-start) | collective-permute-done | bytes 8224 | tf_op jit(solution)/shard_map/ppermute | solution.py:151
  5.8 2.1 %collective-permute-start.1 = (bf16[64,128]{1,0:T(8,128)(2,1)S(1)}, bf16[64,128]{1,0:T(8,128)(2,1)S(1)}, u32[]{:S(2)}, u32[]{:S(2)}) collective-permute-start(bf16[64,128]{1,0:T(8,128)(2,1)S(1)} %pad_maximum_fusion.2), channel_id=1, source_target_pairs={{0,5},{1,4},{2,7},{3,6},{4,1},{5,0},{6,3},{7,2},{8,13},{9,12},{10,... | collective-permute-start | bytes 49160 | tf_op jit(solution)/shard_map/ppermute | solution.py:151
  7.8 0.4 %collective-permute-start.6 = (bf16[16,16,128]{2,1,0:T(8,128)(2,1)S(1)}, bf16[16,16,128]{2,1,0:T(8,128)(2,1)S(1)}, u32[]{:S(2)}, u32[]{:S(2)}) collective-permute-start(bf16[16,16,128]{2,1,0:T(8,128)(2,1)S(1)} %get-tuple-element.16), channel_id=1, source_target_pairs={{0,1},{1,2},{2,0},{3,4},{4,3},{5,6},{6,5},{7,8},{8,7},{9,10},{10,9... | collective-permute-start | bytes 196616 | tf_op jit(solution)/shard_map/ppermute | solution.py:210
  8.2 1.2 %collective-permute-start.5 = (bf16[16,16,128]{2,1,0:T(8,128)(2,1)S(1)}, bf16[16,16,128]{2,1,0:T(8,128)(2,1)S(1)}, u32[]{:S(2)}, u32[]{:S(2)}) collective-permute-start(bf16[16,16,128]{2,1,0:T(8,128)(2,1)S(1)} %get-tuple-element.16), channel_id=1, source_target_pairs={{0,3},{1,2},{2,1},{3,0},{4,7},{5,6},{6,5},{7,4},{8,11},{9,10},{10,... | collective-permute-start | bytes 196616 | tf_op jit(solution)/shard_map/ppermute | solution.py:151
  9.4 0.6 %collective-permute-start.4 = (bf16[16,16,128]{2,1,0:T(8,128)(2,1)S(1)}, bf16[16,16,128]{2,1,0:T(8,128)(2,1)S(1)}, u32[]{:S(2)}, u32[]{:S(2)}) collective-permute-start(bf16[16,16,128]{2,1,0:T(8,128)(2,1)S(1)} %get-tuple-element.15), channel_id=1, source_target_pairs={{0,1},{1,0},{2,3},{3,2},{4,5},{5,4},{6,7},{7,6},{8,9},{9,8},{10,11... | collective-permute-start | bytes 196616 | tf_op jit(solution)/shard_map/ppermute | solution.py:151
  10.0 0.0 collective-permute-done.1.rest_2_
  10.0 0.0 slice-start
  10.0 0.0 slice-start.1
  10.0 0.0 copy-start
  10.0 0.0 copy-start.1
  10.0 2.3 %collective-permute-start.2 = (bf16[128,128]{1,0:T(8,128)(2,1)S(1)}, bf16[128,128]{1,0:T(8,128)(2,1)S(1)}, u32[]{:S(2)}, u32[]{:S(2)}) collective-permute-start(bf16[128,128]{1,0:T(8,128)(2,1)S(1)} %pad_maximum_fusion.1), channel_id=1, source_target_pairs={{0,9},{1,8},{2,11},{3,10},{4,13},{5,12},{6,15},{7,14},{8,1},{9,0},... | collective-permute-start | bytes 98312 | tf_op jit(solution)/shard_map/ppermute | solution.py:151
  12.3 0.0 copy-done.4
  12.3 0.0 copy-done.3
  12.3 0.7 %weights.1 = (f32[2,32,8,128]{3,2,1,0:T(8,128)S(1)}, s32[32,8,128]{2,1,0:T(8,128)S(1)}) custom-call(s32[32]{0:T(128)S(1)} %copy-done.4, f32[2,32]{1,0:T(2,128)S(1)} %copy-done.3), custom_call_target="tpu_custom_call" | custom-call | flops 99999997952 | bytes 1000000 | tf_op jit(solution)/shard_map/weights/pallas_call | solution.py:224
  13.0 1.5 %collective-permute-done.2.rest_3_ = bf16[128,128]{1,0:T(8,128)(2,1)S(1)} collective-permute-done((bf16[128,128]{1,0:T(8,128)(2,1)S(1)}, bf16[128,128]{1,0:T(8,128)(2,1)S(1)}, u32[]{:S(2)}, u32[]{:S(2)}) %collective-permute-start.2) | collective-permute-done | bytes 32800 | tf_op jit(solution)/shard_map/ppermute | solution.py:151
  14.4 0.1 collective-permute-start.3
  14.6 0.0 collective-permute-done.4.chip_halo
  14.6 0.0 collective-permute-done.6.far_halo
  14.6 0.0 collective-permute-done.5.near_halo
  14.6 0.0 slice-done
  14.6 0.0 slice-done.1
  14.6 0.0 copy-done
  14.6 0.0 copy-done.1
  14.6 0.0 copy-start.2
  14.6 1.5 %shard_map.83.rest_6_ = f32[11,16,128]{2,1,0:T(8,128)S(1)} custom-call(s32[8,32]{1,0:T(8,128)S(1)} %bitcast.3, s32[32]{0:T(128)S(1)} %copy-done.1, bf16[32,16,128]{2,1,0:T(8,128)(2,1)S(1)} %get-tuple-element.14.density, bf16[16,16,128]{2,1,0:T(8,128)(2,1)S(1)} %collective-permute-done.4.chip_halo, bf16[16,16,128]{2,1,0:T(8,128)(2,1)S(1)} %collective-permute-done.5.near_halo, ...), custom_call_target="tpu_custom_call" | custom-call | flops 2000000000 | bytes 1000000 | tf_op jit(solution)/shard_map/pallas_call | solution.py:241
  16.1 2.2 %shard_map.82.rest_5_ = f32[21,16,128]{2,1,0:T(8,128)S(1)} custom-call(s32[8,32]{1,0:T(8,128)S(1)} %bitcast.4, s32[32]{0:T(128)S(1)} %copy-done.1, bf16[32,16,128]{2,1,0:T(8,128)(2,1)S(1)} %get-tuple-element.14.density, bf16[16,16,128]{2,1,0:T(8,128)(2,1)S(1)} %collective-permute-done.4.chip_halo, bf16[16,16,128]{2,1,0:T(8,128)(2,1)S(1)} %collective-permute-done.5.near_halo, ...), custom_call_target="tpu_custom_call" | custom-call | flops 2000000000 | bytes 1000000 | tf_op jit(solution)/shard_map/pallas_call | solution.py:241
  18.3 0.0 collective-permute-done.3.rest_4_
  18.3 0.0 copy-done.2
  18.3 1.1 %far.1 = bf16[32,16,128]{2,1,0:T(8,128)(2,1)} custom-call(f32[2,32,8,128]{3,2,1,0:T(8,128)S(1)} %get-tuple-element.11.weights, s32[32,8,128]{2,1,0:T(8,128)S(1)} %get-tuple-element.12.second, bf16[32,128,128]{2,1,0:T(8,128)(2,1)S(1)} %copy-done.2, bf16[32,128]{1,0:T(8,128)(2,1)S(1)} %get-tuple-element.13.rest_0_, ...), custom_call_target="tpu_custom_call" | custom-call | flops 1000000000 | bytes 1000000 | tf_op jit(solution)/shard_map/far/pallas_call | solution.py:243
  (4 shorter events, 0.0 us)
Async XLA Ops:
  0.0 12.3 %copy-start.4 = (s32[32]{0:T(128)S(1)}, s32[32]{0:T(128)}, u32[]{:S(2)}) copy-start(s32[32]{0:T(128)} %coarse_in.1) | copy-start | bytes 388
  0.0 12.3 %copy-start.3 = (f32[2,32]{1,0:T(2,128)S(1)}, f32[2,32]{1,0:T(2,128)}, u32[]{:S(2)}) copy-start(f32[2,32]{1,0:T(2,128)} %coupling.1) | copy-start | bytes 772
  1.9 3.9 %collective-permute-start = (bf16[32,128]{1,0:T(8,128)(2,1)S(1)}, bf16[32,128]{1,0:T(8,128)(2,1)S(1)}, u32[]{:S(2)}, u32[]{:S(2)}) collective-permute-start(bf16[32,128]{1,0:T(8,128)(2,1)S(1)} %get-tuple-element.13.rest_0_), channel_id=1, source_target_pairs={{0,3},{1,2},{2,1},{3,0},{4,7},{5,6},{6,5},{7,4},{8,11},{9,10},{10,... | collective-permute-start | bytes 24584 | tf_op jit(solution)/shard_map/ppermute | solution.py:151
  5.8 4.2 %collective-permute-start.1 = (bf16[64,128]{1,0:T(8,128)(2,1)S(1)}, bf16[64,128]{1,0:T(8,128)(2,1)S(1)}, u32[]{:S(2)}, u32[]{:S(2)}) collective-permute-start(bf16[64,128]{1,0:T(8,128)(2,1)S(1)} %pad_maximum_fusion.2), channel_id=1, source_target_pairs={{0,5},{1,4},{2,7},{3,6},{4,1},{5,0},{6,3},{7,2},{8,13},{9,12},{10,... | collective-permute-start | bytes 49160 | tf_op jit(solution)/shard_map/ppermute | solution.py:151
  7.8 6.7 %collective-permute-start.6 = (bf16[16,16,128]{2,1,0:T(8,128)(2,1)S(1)}, bf16[16,16,128]{2,1,0:T(8,128)(2,1)S(1)}, u32[]{:S(2)}, u32[]{:S(2)}) collective-permute-start(bf16[16,16,128]{2,1,0:T(8,128)(2,1)S(1)} %get-tuple-element.16), channel_id=1, source_target_pairs={{0,1},{1,2},{2,0},{3,4},{4,3},{5,6},{6,5},{7,8},{8,7},{9,10},{10,9... | collective-permute-start | bytes 196616 | tf_op jit(solution)/shard_map/ppermute | solution.py:210
  8.2 6.3 %collective-permute-start.5 = (bf16[16,16,128]{2,1,0:T(8,128)(2,1)S(1)}, bf16[16,16,128]{2,1,0:T(8,128)(2,1)S(1)}, u32[]{:S(2)}, u32[]{:S(2)}) collective-permute-start(bf16[16,16,128]{2,1,0:T(8,128)(2,1)S(1)} %get-tuple-element.16), channel_id=1, source_target_pairs={{0,3},{1,2},{2,1},{3,0},{4,7},{5,6},{6,5},{7,4},{8,11},{9,10},{10,... | collective-permute-start | bytes 196616 | tf_op jit(solution)/shard_map/ppermute | solution.py:151
  9.4 5.1 %collective-permute-start.4 = (bf16[16,16,128]{2,1,0:T(8,128)(2,1)S(1)}, bf16[16,16,128]{2,1,0:T(8,128)(2,1)S(1)}, u32[]{:S(2)}, u32[]{:S(2)}) collective-permute-start(bf16[16,16,128]{2,1,0:T(8,128)(2,1)S(1)} %get-tuple-element.15), channel_id=1, source_target_pairs={{0,1},{1,0},{2,3},{3,2},{4,5},{5,4},{6,7},{7,6},{8,9},{9,8},{10,11... | collective-permute-start | bytes 196616 | tf_op jit(solution)/shard_map/ppermute | solution.py:151
  10.0 4.6 %slice-start = ((s8[8388608]{0:T(1024)(128)(4,1)}), s8[4194304]{0:T(1024)(128)(4,1)S(1)}, s32[]{:S(2)}) async-start(s8[8388608]{0:T(1024)(128)(4,1)} %bitcast.1), calls=%async_computation | async-start | bytes 8388608
  10.0 4.6 %slice-start.1 = ((s8[8388608]{0:T(1024)(128)(4,1)}), s8[4194304]{0:T(1024)(128)(4,1)S(1)}, s32[]{:S(2)}) async-start(s8[8388608]{0:T(1024)(128)(4,1)} %bitcast.1), calls=%async_computation.1 | async-start | bytes 8388608
  10.0 4.6 %copy-start = (s32[32,8]{0,1:T(8,128)S(1)}, s32[32,8]{0,1:T(8,128)}, u32[]{:S(2)}) copy-start(s32[32,8]{0,1:T(8,128)} %param.10) | copy-start | bytes 3076
  10.0 4.6 %copy-start.1 = (s32[32]{0:T(128)S(1)}, s32[32]{0:T(128)}, u32[]{:S(2)}) copy-start(s32[32]{0:T(128)} %counts.3) | copy-start | bytes 388
  10.0 4.4 %collective-permute-start.2 = (bf16[128,128]{1,0:T(8,128)(2,1)S(1)}, bf16[128,128]{1,0:T(8,128)(2,1)S(1)}, u32[]{:S(2)}, u32[]{:S(2)}) collective-permute-start(bf16[128,128]{1,0:T(8,128)(2,1)S(1)} %pad_maximum_fusion.1), channel_id=1, source_target_pairs={{0,9},{1,8},{2,11},{3,10},{4,13},{5,12},{6,15},{7,14},{8,1},{9,0},... | collective-permute-start | bytes 98312 | tf_op jit(solution)/shard_map/ppermute | solution.py:151
  14.4 3.8 %collective-permute-start.3 = (bf16[256,128]{1,0:T(8,128)(2,1)S(1)}, bf16[256,128]{1,0:T(8,128)(2,1)S(1)}, u32[]{:S(2)}, u32[]{:S(2)}) collective-permute-start(bf16[256,128]{1,0:T(8,128)(2,1)S(1)} %pad_maximum_fusion), channel_id=1, source_target_pairs={{0,1},{1,0},{2,3},{3,2},{4,5},{5,4},{6,7},{7,6},{8,9},{9,8},{10,11... | collective-permute-start | bytes 196616 | tf_op jit(solution)/shard_map/ppermute | solution.py:151
  14.6 3.7 %copy-start.2 = (bf16[32,128,128]{2,1,0:T(8,128)(2,1)S(1)}, bf16[32,128,128]{2,1,0:T(8,128)(2,1)}, u32[]{:S(2)}) copy-start(bf16[32,128,128]{2,1,0:T(8,128)(2,1)} %evaluate.1) | copy-start | bytes 3145732

commit v2 on v1

v2 whole, which is shorter than its diff:
```python
import functools

import jax
import jax.numpy as jnp
from jax import lax
from jax.experimental import pallas as pl
from jax.experimental.pallas import tpu as pltpu
from jax.sharding import PartitionSpec as P

F32 = jnp.float32
BF16 = jnp.bfloat16
VMEM = pl.BlockSpec(memory_space=pltpu.VMEM)
HBM = pl.BlockSpec(memory_space=pltpu.HBM)
SMEM = pl.BlockSpec(memory_space=pltpu.SMEM)
NT = (((1,), (1,)), ((), ()))
NN = (((1,), (0,)), ((), ()))


def moments_kernel(chunks, coarse_in, density_in, restrict_in, out, kept, to_chip, to_off, coarse, restrict, masked, sems):
    blk_count, columns, panels = density_in.shape
    groups = out.shape[0] // columns
    half = to_chip.shape[0]
    size = blk_count // chunks
    position = lax.axis_index("panel")
    odd = lax.rem(position, 2)
    first = position * groups
    copies = [
        pltpu.make_async_copy(density_in, kept, sems.at[0]),
        pltpu.make_async_copy(coarse_in, coarse, sems.at[1]),
    ]
    for i in range(chunks):
        part = pl.ds(i * size, size)
        copies.append(pltpu.make_async_copy(restrict_in.at[part], restrict.at[part], sems.at[2 + i]))
    for copy in copies:
        copy.start()
    copies[0].wait()
    to_chip[...] = kept[pl.ds((1 - odd) * half, half)]
    to_off[...] = kept[pl.ds(odd * half, half)]
    copies[1].wait()
    for b in range(blk_count):
        block = kept[b]
        for c in range(groups):
            here = (coarse[b] - first) == c
            rows, lanes = slice(c * columns, (c + 1) * columns), slice(b * panels, (b + 1) * panels)
            masked[rows, lanes] = jnp.where(here, block, jnp.zeros_like(block))
    total = None
    for i in range(chunks):
        copies[2 + i].wait()
        right = jnp.concatenate([restrict[b] for b in range(i * size, (i + 1) * size)], axis=1)
        left = masked[:, i * size * panels : (i + 1) * size * panels]
        part = lax.dot_general(left, right, NT, preferred_element_type=F32)
        total = part if total is None else total + part
    out[...] = total.astype(out.dtype)


def near_kernel(on, ids, counts, density, *rest):
    halos, (blocks, out, extended) = rest[:-3], rest[-3:]
    blk_count, columns, panels = density.shape
    half = out.shape[0]
    slots = ids.shape[0]
    position = lax.axis_index("panel")
    odd = lax.rem(position, 2)
    base = (1 - odd) * half if on else odd * half
    low = odd if on else 1 - odd
    if on:
        halo = halos[0][...]
    else:
        quarter = lax.rem(position, 4)
        middle = jnp.logical_or(quarter == 1, quarter == 2)
        halo = jnp.where(middle, halos[0][...], halos[1][...])
    extended[pl.ds(half, blk_count)] = density[...]
    extended[pl.ds((1 - low) * (half + blk_count), half)] = halo
    empty = blk_count + 2 * half
    extended[empty] = jnp.zeros((columns, panels), extended.dtype)
    live = lax.broadcasted_iota(jnp.int32, ids.shape, 0) < counts[...]
    slabs = jnp.where(live, ids[...] - (position * blk_count - half), empty)
    slabs = jnp.where(base == 0, slabs[:, :half], slabs[:, half:])
    for at in range(half):
        b = base + at
        left = jnp.concatenate([extended[slabs[j, at]] for j in range(slots)], axis=1)
        right = jnp.concatenate([blocks[b, j] for j in range(slots)], axis=1)
        out[at] = lax.dot_general(left, right, NT, preferred_element_type=F32)


def weights_kernel(masks, coarse, coupling, weights, second):
    groups = coupling.shape[0]
    position = lax.axis_index("panel")
    tile = weights.shape[2:]
    columns = coupling[...]
    where_from = lax.broadcasted_iota(jnp.int32, columns.shape, 1)
    for s, mask in enumerate(masks):
        source = lax.bitwise_xor(position, mask) * groups
        for g in range(groups):
            one = jnp.sum(jnp.where(where_from == source + g, columns, 0.0), axis=1, keepdims=True)
            for c in range(groups):
                weights[c, s * groups + g] = jnp.broadcast_to(one[c : c + 1], tile)
    own = coarse[...] - position * groups
    for b in range(second.shape[0]):
        second[b] = jnp.broadcast_to(own[:, b : b + 1], tile)


def far_kernel(parts, weights, second, evaluate, *rest):
    moments, near, out = rest[:parts], rest[parts:-1], rest[-1]
    blk_count, columns, panels = out.shape
    groups, _ = weights.shape[:2]
    local = []
    for c in range(groups):
        total = jnp.zeros((columns, panels), F32)
        s = 0
        for piece in moments:
            for at in range(0, piece.shape[0], columns):
                row = piece[pl.ds(at, columns)].astype(F32)
                weight = weights[c, s]
                total += row * jnp.concatenate([weight] * (columns // weight.shape[0]), axis=0)
                s += 1
        local.append(total.astype(BF16))
    left = jnp.concatenate(local, axis=0)
    half = blk_count // 2
    odd = lax.rem(lax.axis_index("panel"), 2)
    for base, part in (((1 - odd) * half, near[0]), (odd * half, near[1])):
        for at in range(0, half, 2):
            right = jnp.concatenate([evaluate[base + at], evaluate[base + at + 1]], axis=1)
            both = lax.dot_general(left, right, NN, preferred_element_type=F32)
            for i in (0, 1):
                b = base + at + i
                pick = jnp.concatenate([second[b]] * (columns // second.shape[1]), axis=0)
                lanes = slice(i * panels, (i + 1) * panels)
                far = both[:columns, lanes]
                for c in range(1, groups):
                    far = jnp.where(pick == c, both[c * columns : (c + 1) * columns, lanes], far)
                out[b] = (part[at + i] + far).astype(out.dtype)


def on_chip(*arrays):
    return [pltpu.with_memory_space_constraint(x, pltpu.VMEM) for x in arrays]


def in_hbm(*arrays):
    return [pltpu.with_memory_space_constraint(x, pltpu.HBM) for x in arrays]


def room(mebibytes):
    return pltpu.CompilerParams(vmem_limit_bytes=mebibytes << 20)


def cost(flops, moved):
    return pl.CostEstimate(flops=flops, bytes_accessed=moved, transcendentals=0)


def exchange(x, step):
    count = lax.axis_size("panel")
    return lax.ppermute(x, "panel", [(i, i ^ step) for i in range(count)])


def far_pairs(count):
    goes = {}
    for i in range(3, count - 1, 4):
        goes[i], goes[i + 1] = i + 1, i
    for i in range(5, count - 4, 4):
        goes[i], goes[i + 1] = i + 1, i
    for base in (0, count - 3):
        for i in range(3):
            goes[base + i] = base + (i + 1) % 3
    return sorted(goes.items())


def body(density, near_blocks, neighbours, counts, coarse_map, restrict, evaluate, coupling):
    blk_count, columns, panels = density.shape
    terms = restrict.shape[1]
    groups = coupling.shape[0]
    half = blk_count // 2
    count = lax.axis_size("panel")
    position = lax.axis_index("panel")
    odd = lax.rem(position, 2)

    bits = list(range(count.bit_length() - 2, 0, -1))
    steps = [(1 << bit) | 1 for bit in bits[:1] + bits[-1:] + bits[1:-1]] + [1]
    masks = [0]
    for step in steps:
        masks = masks + [mask ^ step for mask in masks]

    half_shape = (half, columns, panels)
    chunks = 1
    moments, kept, to_chip, to_off = pl.pallas_call(
        functools.partial(moments_kernel, chunks),
        out_shape=(
            pltpu.VMEM((groups * columns, terms), BF16),
            pltpu.VMEM(density.shape, BF16),
            pltpu.VMEM(half_shape, BF16),
            pltpu.VMEM(half_shape, BF16),
        ),
        in_specs=[HBM] * 3,
        out_specs=(VMEM,) * 4,
        scratch_shapes=[
            pltpu.SMEM(coarse_map.shape, jnp.int32),
            pltpu.VMEM(restrict.shape, BF16),
            pltpu.VMEM((groups * columns, blk_count * panels), BF16),
            pltpu.SemaphoreType.DMA((2 + chunks,)),
        ],
        compiler_params=room(8),
        cost_estimate=cost(10**10, 10**6),
        name="moments",
    )(*in_hbm(coarse_map, density, restrict))

    pieces = [moments]
    for at, step in enumerate(steps):
        sent = pieces[0] if at == 0 else jnp.concatenate(pieces, axis=0)
        pieces.append(exchange(sent, step))

    chip_halo = exchange(to_chip, 1)
    near_halo = exchange(to_off, 3)
    to_far = to_off
    far_halo = lax.ppermute(to_far, "panel", far_pairs(count))

    make_weights = pl.pallas_call(
        functools.partial(weights_kernel, masks),
        out_shape=(
            pltpu.VMEM((groups, groups * count, 8, 128), F32),
            pltpu.VMEM((blk_count, 8, 128), jnp.int32),
        ),
        in_specs=[VMEM, VMEM],
        out_specs=(VMEM, VMEM),
        compiler_params=room(4),
        cost_estimate=cost(10**11, 10**6),
        name="weights",
    )
    weights, second = make_weights(*on_chip(coarse_map.reshape(1, blk_count), coupling))

    ids = neighbours.T
    live_counts = counts.reshape(1, blk_count)
    near = []
    for on, halos in ((True, (chip_halo,)), (False, (near_halo, far_halo))):
        call = pl.pallas_call(
            functools.partial(near_kernel, on),
            out_shape=pltpu.VMEM((half, columns, panels), F32),
            in_specs=[VMEM] * (4 + len(halos)),
            out_specs=VMEM,
            scratch_shapes=[
                pltpu.VMEM((blk_count + 2 * half + 1, columns, panels), BF16),
            ],
            compiler_params=room(4),
            cost_estimate=cost(2 * 10**9, 10**6),
        )
        near.append(call(*on_chip(ids, live_counts, kept, *halos, near_blocks)))

    return pl.pallas_call(
        functools.partial(far_kernel, len(pieces)),
        out_shape=jax.ShapeDtypeStruct(density.shape, BF16),
        in_specs=[VMEM] * (3 + len(pieces) + len(near)),
        out_specs=VMEM,
        compiler_params=room(4),
        cost_estimate=cost(10**9, 10**6),
        name="far",
    )(*on_chip(weights, second, evaluate, *pieces, *near))


def solution(mesh):
    placed = (
        P(("grp", "panel"), None, None),
        P(("grp", "panel"), None, None, None),
        P(("grp", "panel"), None),
        P(("grp", "panel")),
        P(("grp", "panel")),
        P(("grp", "panel"), None, None),
        P(("grp", "panel"), None, None),
        P(("grp", "panel"), None),
    )
    return jax.shard_map(
        body,
        mesh=mesh,
        in_specs=placed,
        out_specs=P(("grp", "panel"), None, None),
        check_vma=False,
    )
```

time: 19.6 us -> 19.3 us (0.985)
  Pallas kernels: 7.32 us -> 5.84 us
  starting transfers between devices: 9.08 us -> 10.4 us
    pallas_call x3, Pallas kernels: 4.32 us -> 2.92 us  [the longest x2 2.72 us: body(): near.append(call(*on_chip(ids, live_counts, kept, *halos, near_blocks)))]
    ppermute x6, starting transfers between devices: 8.69 us -> 9.96 us  [exchange(): return lax.ppermute(x, 'panel', [(i, i ^ step) for i in range(count)])]
  transfers between devices with their start and end apart: 7 -> 7, of which waited for: 2 -> 2; matrix products, arithmetic and copies ran while one was open for 0% -> 0% of each run, Pallas kernels for 22% -> 15%
where the time goes in v2:
time: 19.3 us; the launch traced here: 19.2 us
  starting transfers between devices  10.4 us (54%)
  Pallas kernels  5.84 us (30%)
  waiting for transfers between devices  2.8 us (15%)
    ppermute x6, starting transfers between devices, exchange(): return lax.ppermute(x, 'panel', [(i, i ^ step) for i in range(count)])  9.96 us
    ppermute x6, waiting for transfers between devices, exchange(): return lax.ppermute(x, 'panel', [(i, i ^ step) for i in range(count)])  2.8 us
    pallas_call x2, Pallas kernels, body(): near.append(call(*on_chip(ids, live_counts, kept, *halos, near_blocks)))  2.72 us
    pallas_call x1, Pallas kernels, body(): pl.pallas_call(functools.partial(moments_kernel, chunks), out_shape=(pltp...  1.91 us
    pallas_call x1, Pallas kernels, body(): pl.pallas_call(functools.partial(far_kernel, len(pieces)), out_shape=jax....  1.01 us
    ppermute x1, starting transfers between devices, body(): far_halo = lax.ppermute(to_far, 'panel', far_pairs(count))  0.4 us
  transfers between devices with their start and end apart: 7, of which 2 were waited for; matrix products, arithmetic and copies ran while one was open for 0% of the time, Pallas kernels for 15%

profile of v2, /device:TPU:0, one launch (start us, length us, event | category | flops | bytes accessed | tf_op | source)
XLA Modules:
  0.0 19.2 jit_solution(12213227001542528727)
XLA Ops:
  0.0 0.0 copy-start.4
  0.0 0.0 copy-start.3
  0.0 0.0 slice-start
  0.0 1.9 %moments.1 = (bf16[32,128]{1,0:T(8,128)(2,1)S(1)}, bf16[32,16,128]{2,1,0:T(8,128)(2,1)S(1)}, bf16[16,16,128]{2,1,0:T(8,128)(2,1)S(1)}, bf16[16,16,128]{2,1,0:T(8,128)(2,1)S(1)}) custom-call(s32[32]{0:T(128)} %coarse_in.1, bf16[32,16,128]{2,1,0:T(8,128)(2,1)} %density_in.1, bf16[32,128,128]{2,1,0:T(8,128)(2,1)} %restrict_in.1), custom_call_target="tpu_custom_call" | custom-call | flops 10000000000 | bytes 1000000 | tf_op jit(solution)/shard_map/moments/pallas_call | solution.py:184
  1.9 3.6 %collective-permute-start = (bf16[32,128]{1,0:T(8,128)(2,1)S(1)}, bf16[32,128]{1,0:T(8,128)(2,1)S(1)}, u32[]{:S(2)}, u32[]{:S(2)}) collective-permute-start(bf16[32,128]{1,0:T(8,128)(2,1)S(1)} %get-tuple-element.13.rest_0_), channel_id=1, source_target_pairs={{0,9},{1,8},{2,11},{3,10},{4,13},{5,12},{6,15},{7,14},{8,1},{9,0},... | collective-permute-start | bytes 24584 | tf_op jit(solution)/shard_map/ppermute | solution.py:152
  5.5 1.4 %collective-permute-done.rest_1_ = bf16[32,128]{1,0:T(8,128)(2,1)S(1)} collective-permute-done((bf16[32,128]{1,0:T(8,128)(2,1)S(1)}, bf16[32,128]{1,0:T(8,128)(2,1)S(1)}, u32[]{:S(2)}, u32[]{:S(2)}) %collective-permute-start) | collective-permute-done | bytes 8224 | tf_op jit(solution)/shard_map/ppermute | solution.py:152
  6.9 1.8 %collective-permute-start.1 = (bf16[64,128]{1,0:T(8,128)(2,1)S(1)}, bf16[64,128]{1,0:T(8,128)(2,1)S(1)}, u32[]{:S(2)}, u32[]{:S(2)}) collective-permute-start(bf16[64,128]{1,0:T(8,128)(2,1)S(1)} %pad_maximum_fusion.2), channel_id=1, source_target_pairs={{0,3},{1,2},{2,1},{3,0},{4,7},{5,6},{6,5},{7,4},{8,11},{9,10},{10,... | collective-permute-start | bytes 49160 | tf_op jit(solution)/shard_map/ppermute | solution.py:152
  8.7 0.4 %collective-permute-start.6 = (bf16[16,16,128]{2,1,0:T(8,128)(2,1)S(1)}, bf16[16,16,128]{2,1,0:T(8,128)(2,1)S(1)}, u32[]{:S(2)}, u32[]{:S(2)}) collective-permute-start(bf16[16,16,128]{2,1,0:T(8,128)(2,1)S(1)} %get-tuple-element.16), channel_id=1, source_target_pairs={{0,1},{1,2},{2,0},{3,4},{4,3},{5,6},{6,5},{7,8},{8,7},{9,10},{10,9... | collective-permute-start | bytes 196616 | tf_op jit(solution)/shard_map/ppermute | solution.py:213
  9.1 2.4 %collective-permute-start.5 = (bf16[16,16,128]{2,1,0:T(8,128)(2,1)S(1)}, bf16[16,16,128]{2,1,0:T(8,128)(2,1)S(1)}, u32[]{:S(2)}, u32[]{:S(2)}) collective-permute-start(bf16[16,16,128]{2,1,0:T(8,128)(2,1)S(1)} %get-tuple-element.16), channel_id=1, source_target_pairs={{0,3},{1,2},{2,1},{3,0},{4,7},{5,6},{6,5},{7,4},{8,11},{9,10},{10,... | collective-permute-start | bytes 196616 | tf_op jit(solution)/shard_map/ppermute | solution.py:152
  11.5 0.0 collective-permute-start.4
  11.5 0.0 collective-permute-done.1.rest_2_
  11.5 1.8 %collective-permute-start.2 = (bf16[128,128]{1,0:T(8,128)(2,1)S(1)}, bf16[128,128]{1,0:T(8,128)(2,1)S(1)}, u32[]{:S(2)}, u32[]{:S(2)}) collective-permute-start(bf16[128,128]{1,0:T(8,128)(2,1)S(1)} %pad_maximum_fusion.1), channel_id=1, source_target_pairs={{0,5},{1,4},{2,7},{3,6},{4,1},{5,0},{6,3},{7,2},{8,13},{9,12},{10,... | collective-permute-start | bytes 98312 | tf_op jit(solution)/shard_map/ppermute | solution.py:152
  13.2 0.0 copy-done.4
  13.2 0.0 copy-done.3
  13.2 0.0 slice-start.1
  13.2 0.0 copy-start
  13.2 0.0 copy-start.1
  13.3 0.2 %weights.1 = (f32[2,32,8,128]{3,2,1,0:T(8,128)S(1)}, s32[32,8,128]{2,1,0:T(8,128)S(1)}) custom-call(s32[1,32]{1,0:T(1,128)S(1)} %bitcast.9, f32[2,32]{1,0:T(2,128)S(1)} %copy-done.3), custom_call_target="tpu_custom_call" | custom-call | flops 99999997952 | bytes 1000000 | tf_op jit(solution)/shard_map/weights/pallas_call | solution.py:227
  13.4 1.4 %collective-permute-done.2.rest_3_ = bf16[128,128]{1,0:T(8,128)(2,1)S(1)} collective-permute-done((bf16[128,128]{1,0:T(8,128)(2,1)S(1)}, bf16[128,128]{1,0:T(8,128)(2,1)S(1)}, u32[]{:S(2)}, u32[]{:S(2)}) %collective-permute-start.2) | collective-permute-done | bytes 32800 | tf_op jit(solution)/shard_map/ppermute | solution.py:152
  14.9 0.4 %collective-permute-start.3 = (bf16[256,128]{1,0:T(8,128)(2,1)S(1)}, bf16[256,128]{1,0:T(8,128)(2,1)S(1)}, u32[]{:S(2)}, u32[]{:S(2)}) collective-permute-start(bf16[256,128]{1,0:T(8,128)(2,1)S(1)} %pad_maximum_fusion), channel_id=1, source_target_pairs={{0,1},{1,0},{2,3},{3,2},{4,5},{5,4},{6,7},{7,6},{8,9},{9,8},{10,11... | collective-permute-start | bytes 196616 | tf_op jit(solution)/shard_map/ppermute | solution.py:152
  15.3 0.0 collective-permute-done.4.rest_0_
  15.3 0.0 slice-done
  15.3 0.1 slice-done.1
  15.4 0.0 copy-done
  15.4 0.0 copy-done.1
  15.4 0.0 copy-start.2
  15.4 1.3 %shard_map.82.rest_5_ = f32[16,16,128]{2,1,0:T(8,128)S(1)} custom-call(s32[8,32]{1,0:T(8,128)S(1)} %bitcast.5, s32[1,32]{1,0:T(1,128)S(1)} %bitcast.7, bf16[32,16,128]{2,1,0:T(8,128)(2,1)S(1)} %get-tuple-element.14.density, bf16[16,16,128]{2,1,0:T(8,128)(2,1)S(1)} %collective-permute-done.4.rest_0_, bf16[32,8,128,128]{3,2,1,0:T(8,128)(2,1)S(1)} %bitcast.4), custom_call_target="tpu_custom_call" | custom-call | flops 2000000000 | bytes 1000000 | tf_op jit(solution)/shard_map/pallas_call | solution.py:244
  16.8 0.0 collective-permute-done.6.rest_1_
  16.8 0.0 collective-permute-done.5.rest_0_
  16.8 1.4 %shard_map.83.rest_6_ = f32[16,16,128]{2,1,0:T(8,128)S(1)} custom-call(s32[8,32]{1,0:T(8,128)S(1)} %bitcast.6, s32[1,32]{1,0:T(1,128)S(1)} %bitcast.8, bf16[32,16,128]{2,1,0:T(8,128)(2,1)S(1)} %get-tuple-element.14.density, bf16[16,16,128]{2,1,0:T(8,128)(2,1)S(1)} %collective-permute-done.5.rest_0_, bf16[16,16,128]{2,1,0:T(8,128)(2,1)S(1)} %collective-permute-done.6.rest_1_, ...), custom_call_target="tpu_custom_call" | custom-call | flops 2000000000 | bytes 1000000 | tf_op jit(solution)/shard_map/pallas_call | solution.py:244
  18.2 0.0 collective-permute-done.3.rest_4_
  18.2 0.0 copy-done.2
  18.2 1.0 %far.1 = bf16[32,16,128]{2,1,0:T(8,128)(2,1)} custom-call(f32[2,32,8,128]{3,2,1,0:T(8,128)S(1)} %get-tuple-element.11.weights, s32[32,8,128]{2,1,0:T(8,128)S(1)} %get-tuple-element.12.second, bf16[32,128,128]{2,1,0:T(8,128)(2,1)S(1)} %copy-done.2, bf16[32,128]{1,0:T(8,128)(2,1)S(1)} %get-tuple-element.13.rest_0_, ...), custom_call_target="tpu_custom_call" | custom-call | flops 1000000000 | bytes 1000000 | tf_op jit(solution)/shard_map/far/pallas_call | solution.py:246
  (4 shorter events, 0.0 us)
Async XLA Ops:
  0.0 13.2 %copy-start.4 = (s32[32]{0:T(128)S(1)}, s32[32]{0:T(128)}, u32[]{:S(2)}) copy-start(s32[32]{0:T(128)} %coarse_in.1) | copy-start | bytes 388
  0.0 13.2 %copy-start.3 = (f32[2,32]{1,0:T(2,128)S(1)}, f32[2,32]{1,0:T(2,128)}, u32[]{:S(2)}) copy-start(f32[2,32]{1,0:T(2,128)} %coupling.1) | copy-start | bytes 772
  0.0 15.3 %slice-start = ((s8[8388608]{0:T(1024)(128)(4,1)}), s8[4194304]{0:T(1024)(128)(4,1)S(1)}, s32[]{:S(2)}) async-start(s8[8388608]{0:T(1024)(128)(4,1)} %bitcast.3), calls=%async_computation | async-start | bytes 8388608
  1.9 4.9 %collective-permute-start = (bf16[32,128]{1,0:T(8,128)(2,1)S(1)}, bf16[32,128]{1,0:T(8,128)(2,1)S(1)}, u32[]{:S(2)}, u32[]{:S(2)}) collective-permute-start(bf16[32,128]{1,0:T(8,128)(2,1)S(1)} %get-tuple-element.13.rest_0_), channel_id=1, source_target_pairs={{0,9},{1,8},{2,11},{3,10},{4,13},{5,12},{6,15},{7,14},{8,1},{9,0},... | collective-permute-start | bytes 24584 | tf_op jit(solution)/shard_map/ppermute | solution.py:152
  6.9 4.6 %collective-permute-start.1 = (bf16[64,128]{1,0:T(8,128)(2,1)S(1)}, bf16[64,128]{1,0:T(8,128)(2,1)S(1)}, u32[]{:S(2)}, u32[]{:S(2)}) collective-permute-start(bf16[64,128]{1,0:T(8,128)(2,1)S(1)} %pad_maximum_fusion.2), channel_id=1, source_target_pairs={{0,3},{1,2},{2,1},{3,0},{4,7},{5,6},{6,5},{7,4},{8,11},{9,10},{10,... | collective-permute-start | bytes 49160 | tf_op jit(solution)/shard_map/ppermute | solution.py:152
  8.7 8.1 %collective-permute-start.6 = (bf16[16,16,128]{2,1,0:T(8,128)(2,1)S(1)}, bf16[16,16,128]{2,1,0:T(8,128)(2,1)S(1)}, u32[]{:S(2)}, u32[]{:S(2)}) collective-permute-start(bf16[16,16,128]{2,1,0:T(8,128)(2,1)S(1)} %get-tuple-element.16), channel_id=1, source_target_pairs={{0,1},{1,2},{2,0},{3,4},{4,3},{5,6},{6,5},{7,8},{8,7},{9,10},{10,9... | collective-permute-start | bytes 196616 | tf_op jit(solution)/shard_map/ppermute | solution.py:213
  9.1 7.7 %collective-permute-start.5 = (bf16[16,16,128]{2,1,0:T(8,128)(2,1)S(1)}, bf16[16,16,128]{2,1,0:T(8,128)(2,1)S(1)}, u32[]{:S(2)}, u32[]{:S(2)}) collective-permute-start(bf16[16,16,128]{2,1,0:T(8,128)(2,1)S(1)} %get-tuple-element.16), channel_id=1, source_target_pairs={{0,3},{1,2},{2,1},{3,0},{4,7},{5,6},{6,5},{7,4},{8,11},{9,10},{10,... | collective-permute-start | bytes 196616 | tf_op jit(solution)/shard_map/ppermute | solution.py:152
  11.5 3.9 %collective-permute-start.4 = (bf16[16,16,128]{2,1,0:T(8,128)(2,1)S(1)}, bf16[16,16,128]{2,1,0:T(8,128)(2,1)S(1)}, u32[]{:S(2)}, u32[]{:S(2)}) collective-permute-start(bf16[16,16,128]{2,1,0:T(8,128)(2,1)S(1)} %get-tuple-element.15), channel_id=1, source_target_pairs={{0,1},{1,0},{2,3},{3,2},{4,5},{5,4},{6,7},{7,6},{8,9},{9,8},{10,11... | collective-permute-start | bytes 196616 | tf_op jit(solution)/shard_map/ppermute | solution.py:152
  11.5 3.4 %collective-permute-start.2 = (bf16[128,128]{1,0:T(8,128)(2,1)S(1)}, bf16[128,128]{1,0:T(8,128)(2,1)S(1)}, u32[]{:S(2)}, u32[]{:S(2)}) collective-permute-start(bf16[128,128]{1,0:T(8,128)(2,1)S(1)} %pad_maximum_fusion.1), channel_id=1, source_target_pairs={{0,5},{1,4},{2,7},{3,6},{4,1},{5,0},{6,3},{7,2},{8,13},{9,12},{10,... | collective-permute-start | bytes 98312 | tf_op jit(solution)/shard_map/ppermute | solution.py:152
  13.2 2.2 %slice-start.1 = ((s8[8388608]{0:T(1024)(128)(4,1)}), s8[4194304]{0:T(1024)(128)(4,1)S(1)}, s32[]{:S(2)}) async-start(s8[8388608]{0:T(1024)(128)(4,1)} %bitcast.3), calls=%async_computation.1 | async-start | bytes 8388608
  13.2 2.2 %copy-start = (s32[32,8]{0,1:T(8,128)S(1)}, s32[32,8]{0,1:T(8,128)}, u32[]{:S(2)}) copy-start(s32[32,8]{0,1:T(8,128)} %param.10) | copy-start | bytes 3076
  13.2 2.2 %copy-start.1 = (s32[32]{0:T(128)S(1)}, s32[32]{0:T(128)}, u32[]{:S(2)}) copy-start(s32[32]{0:T(128)} %param.11) | copy-start | bytes 388
  14.9 3.3 %collective-permute-start.3 = (bf16[256,128]{1,0:T(8,128)(2,1)S(1)}, bf16[256,128]{1,0:T(8,128)(2,1)S(1)}, u32[]{:S(2)}, u32[]{:S(2)}) collective-permute-start(bf16[256,128]{1,0:T(8,128)(2,1)S(1)} %pad_maximum_fusion), channel_id=1, source_target_pairs={{0,1},{1,0},{2,3},{3,2},{4,5},{5,4},{6,7},{7,6},{8,9},{9,8},{10,11... | collective-permute-start | bytes 196616 | tf_op jit(solution)/shard_map/ppermute | solution.py:152
  15.4 2.7 %copy-start.2 = (bf16[32,128,128]{2,1,0:T(8,128)(2,1)S(1)}, bf16[32,128,128]{2,1,0:T(8,128)(2,1)}, u32[]{:S(2)}) copy-start(bf16[32,128,128]{2,1,0:T(8,128)(2,1)} %evaluate.1) | copy-start | bytes 3145732

commit v3 on v2

--- a/solution.py
+++ b/solution.py
@@ -53,10 +53,10 @@
     out[...] = total.astype(out.dtype)
 
 
-def near_kernel(on, ids, counts, density, *rest):
+def near_kernel(on, begin, ids, counts, density, *rest):
     halos, (blocks, out, extended) = rest[:-3], rest[-3:]
     blk_count, columns, panels = density.shape
-    half = out.shape[0]
+    half = halos[0].shape[0]
     slots = ids.shape[0]
     position = lax.axis_index("panel")
     odd = lax.rem(position, 2)
@@ -65,9 +65,8 @@
     if on:
         halo = halos[0][...]
     else:
-        quarter = lax.rem(position, 4)
-        middle = jnp.logical_or(quarter == 1, quarter == 2)
-        halo = jnp.where(middle, halos[0][...], halos[1][...])
+        relayed = jnp.logical_or(position == 1, position == lax.axis_size("panel") - 2)
+        halo = jnp.where(relayed, halos[1][...], halos[0][...])
     extended[pl.ds(half, blk_count)] = density[...]
     extended[pl.ds((1 - low) * (half + blk_count), half)] = halo
     empty = blk_count + 2 * half
@@ -75,14 +74,18 @@
     live = lax.broadcasted_iota(jnp.int32, ids.shape, 0) < counts[...]
     slabs = jnp.where(live, ids[...] - (position * blk_count - half), empty)
     slabs = jnp.where(base == 0, slabs[:, :half], slabs[:, half:])
-    for at in range(half):
-        b = base + at
-        left = jnp.concatenate([extended[slabs[j, at]] for j in range(slots)], axis=1)
-        right = jnp.concatenate([blocks[b, j] for j in range(slots)], axis=1)
-        out[at] = lax.dot_general(left, right, NT, preferred_element_type=F32)
-
-
-def weights_kernel(masks, coarse, coupling, weights, second):
+    for at in range(out.shape[0]):
+        b = base + begin + at
+        left = [extended[slabs[j, begin + at]] for j in range(slots)]
+        mid = slots // 2
+        turned = jnp.concatenate([blocks[b, j].T for j in range(mid)], axis=0)
+        plain = jnp.concatenate([blocks[b, j] for j in range(mid, slots)], axis=1)
+        out[at] = lax.dot_general(
+            jnp.concatenate(left[mid:], axis=1), plain, NT, preferred_element_type=F32
+        ) + lax.dot_general(jnp.concatenate(left[:mid], axis=1), turned, NN, preferred_element_type=F32)
+
+
+def weights_kernel(masks, coarse, coupling, mark, weights, second):
     groups = coupling.shape[0]
     position = lax.axis_index("panel")
     tile = weights.shape[2:]
@@ -99,7 +102,11 @@
         second[b] = jnp.broadcast_to(own[:, b : b + 1], tile)
 
 
-def far_kernel(parts, weights, second, evaluate, *rest):
+def mark_kernel(out):
+    out[...] = jnp.zeros_like(out)
+
+
+def far_kernel(cuts, parts, weights, second, evaluate, *rest):
     moments, near, out = rest[:parts], rest[parts:-1], rest[-1]
     blk_count, columns, panels = out.shape
     groups, _ = weights.shape[:2]
@@ -117,8 +124,9 @@
     left = jnp.concatenate(local, axis=0)
     half = blk_count // 2
     odd = lax.rem(lax.axis_index("panel"), 2)
-    for base, part in (((1 - odd) * half, near[0]), (odd * half, near[1])):
-        for at in range(0, half, 2):
+    for (on, begin, end), part in zip(cuts, near):
+        base = ((1 - odd) * half if on else odd * half) + begin
+        for at in range(0, end - begin, 2):
             right = jnp.concatenate([evaluate[base + at], evaluate[base + at + 1]], axis=1)
             both = lax.dot_general(left, right, NN, preferred_element_type=F32)
             for i in (0, 1):
@@ -152,15 +160,10 @@
     return lax.ppermute(x, "panel", [(i, i ^ step) for i in range(count)])
 
 
-def far_pairs(count):
-    goes = {}
-    for i in range(3, count - 1, 4):
+def off_pairs(count):
+    goes = {0: 1, 1: 2, 2: 0, count - 3: count - 1, count - 1: count - 2, count - 2: count - 3}
+    for i in range(3, count - 4, 2):
         goes[i], goes[i + 1] = i + 1, i
-    for i in range(5, count - 4, 4):
-        goes[i], goes[i + 1] = i + 1, i
-    for base in (0, count - 3):
-        for i in range(3):
-            goes[base + i] = base + (i + 1) % 3
     return sorted(goes.items())
 
 
@@ -173,11 +176,10 @@
     position = lax.axis_index("panel")
     odd = lax.rem(position, 2)
 
-    bits = list(range(count.bit_length() - 2, 0, -1))
-    steps = [(1 << bit) | 1 for bit in bits[:1] + bits[-1:] + bits[1:-1]] + [1]
+    rounds = rounds_of(count)
     masks = [0]
-    for step in steps:
-        masks = masks + [mask ^ step for mask in masks]
+    for together in rounds:
+        masks = masks + [mask ^ step for step in together for mask in masks]
 
     half_shape = (half, columns, panels)
     chunks = 1
@@ -203,36 +205,47 @@
     )(*in_hbm(coarse_map, density, restrict))
 
     pieces = [moments]
-    for at, step in enumerate(steps):
+    for at, together in enumerate(rounds):
         sent = pieces[0] if at == 0 else jnp.concatenate(pieces, axis=0)
-        pieces.append(exchange(sent, step))
+        for step in together:
+            pieces.append(exchange(sent, step))
 
     chip_halo = exchange(to_chip, 1)
-    near_halo = exchange(to_off, 3)
-    to_far = to_off
-    far_halo = lax.ppermute(to_far, "panel", far_pairs(count))
-
+    off_halo = lax.ppermute(to_off, "panel", off_pairs(count))
+    relay = exchange(off_halo, 1)
+
+    make_mark = pl.pallas_call(
+        mark_kernel,
+        out_shape=pltpu.VMEM((8, 128), F32),
+        out_specs=VMEM,
+        compiler_params=room(1),
+        cost_estimate=cost(10**11, 10**6),
+        name="mark",
+    )
+    mark = make_mark()
     make_weights = pl.pallas_call(
         functools.partial(weights_kernel, masks),
         out_shape=(
             pltpu.VMEM((groups, groups * count, 8, 128), F32),
             pltpu.VMEM((blk_count, 8, 128), jnp.int32),
         ),
-        in_specs=[VMEM, VMEM],
+        in_specs=[VMEM] * 3,
         out_specs=(VMEM, VMEM),
         compiler_params=room(4),
-        cost_estimate=cost(10**11, 10**6),
+        cost_estimate=cost(10**9, 10**6),
         name="weights",
     )
-    weights, second = make_weights(*on_chip(coarse_map.reshape(1, blk_count), coupling))
+    weights, second = make_weights(*on_chip(coarse_map.reshape(1, blk_count), coupling, mark))
 
     ids = neighbours.T
     live_counts = counts.reshape(1, blk_count)
     near = []
-    for on, halos in ((True, (chip_halo,)), (False, (near_halo, far_halo))):
+    cuts = [(on, begin * half // 8, end * half // 8) for on, begin, end in CUTS]
+    for on, begin, end in cuts:
+        halos = (chip_halo,) if on else (off_halo, relay)
         call = pl.pallas_call(
-            functools.partial(near_kernel, on),
-            out_shape=pltpu.VMEM((half, columns, panels), F32),
+            functools.partial(near_kernel, on, begin),
+            out_shape=pltpu.VMEM((end - begin, columns, panels), F32),
             in_specs=[VMEM] * (4 + len(halos)),
             out_specs=VMEM,
             scratch_shapes=[
@@ -244,7 +257,7 @@
         near.append(call(*on_chip(ids, live_counts, kept, *halos, near_blocks)))
 
     return pl.pallas_call(
-        functools.partial(far_kernel, len(pieces)),
+        functools.partial(far_kernel, cuts, len(pieces)),
         out_shape=jax.ShapeDtypeStruct(density.shape, BF16),
         in_specs=[VMEM] * (3 + len(pieces) + len(near)),
         out_specs=VMEM,
@@ -252,6 +265,13 @@
         cost_estimate=cost(10**9, 10**6),
         name="far",
     )(*on_chip(weights, second, evaluate, *pieces, *near))
+
+
+CUTS = ((True, 0, 8), (False, 0, 3), (False, 3, 8))
+
+
+def rounds_of(count):
+    return [[(1 << bit) | 1] for bit in range(count.bit_length() - 2, 2, -1)] + [[6, 3, 5], [1]]
 
 
 def solution(mesh):

time: 19.3 us -> 18.1 us (0.938)
  starting transfers between devices: 10.4 us -> 8.5 us
  waiting for transfers between devices: 2.8 us -> 3.61 us
    ppermute x6 -> x7, starting transfers between devices: 9.96 us -> 8.43 us  [exchange(): return lax.ppermute(x, 'panel', [(i, i ^ step) for i in range(count)])]
    ppermute x6 -> x7, waiting for transfers between devices: 2.8 us -> 3.6 us  [exchange(): return lax.ppermute(x, 'panel', [(i, i ^ step) for i in range(count)])]
    ppermute x1, starting transfers between devices: 0.4 us -> 0.07 us  [body(): off_halo = lax.ppermute(to_off, 'panel', off_pairs(count))]
    pallas_call x2 -> x3, Pallas kernels: 2.72 us -> 2.68 us  [body(): near.append(call(*on_chip(ids, live_counts, kept, *halos, near_blocks)))]
    pallas_call x2 -> x3, Pallas kernels: 1.21 us -> 1.19 us  [the longest x1 0.99 us: body(): pl.pallas_call(functools.partial(far_kernel, cuts, len(pieces)), out_shap...]
  transfers between devices with their start and end apart: 7 -> 8, of which waited for: 2 -> 3; matrix products, arithmetic and copies ran while one was open for 0% -> 0% of each run, Pallas kernels for 15% -> 16%
where the time goes in v3:
time: 18.1 us; the launch traced here: 17.9 us
  starting transfers between devices  8.5 us (47%)
  Pallas kernels  5.65 us (31%)
  waiting for transfers between devices  3.61 us (20%)
    ppermute x7, starting transfers between devices, exchange(): return lax.ppermute(x, 'panel', [(i, i ^ step) for i in range(count)])  8.43 us
    ppermute x7, waiting for transfers between devices, exchange(): return lax.ppermute(x, 'panel', [(i, i ^ step) for i in range(count)])  3.6 us
    pallas_call x3, Pallas kernels, body(): near.append(call(*on_chip(ids, live_counts, kept, *halos, near_blocks)))  2.68 us
    pallas_call x1, Pallas kernels, body(): pl.pallas_call(functools.partial(moments_kernel, chunks), out_shape=(pltp...  1.78 us
    pallas_call x1, Pallas kernels, body(): pl.pallas_call(functools.partial(far_kernel, cuts, len(pieces)), out_shap...  0.99 us
  transfers between devices with their start and end apart: 8, of which 3 were waited for; matrix products, arithmetic and copies ran while one was open for 0% of the time, Pallas kernels for 16%

profile of v3, /device:TPU:0, one launch (start us, length us, event | category | flops | bytes accessed | tf_op | source)
XLA Modules:
  0.0 17.9 jit_solution(2536296373314396458)
XLA Ops:
  0.0 1.8 %moments.1 = (bf16[32,128]{1,0:T(8,128)(2,1)S(1)}, bf16[32,16,128]{2,1,0:T(8,128)(2,1)S(1)}, bf16[16,16,128]{2,1,0:T(8,128)(2,1)S(1)}, bf16[16,16,128]{2,1,0:T(8,128)(2,1)S(1)}) custom-call(s32[32]{0:T(128)} %coarse_in.1, bf16[32,16,128]{2,1,0:T(8,128)(2,1)} %density_in.1, bf16[32,128,128]{2,1,0:T(8,128)(2,1)} %restrict_in.1), custom_call_target="tpu_custom_call" | custom-call | flops 10000000000 | bytes 1000000 | tf_op jit(solution)/shard_map/moments/pallas_call | solution.py:186
  1.8 3.6 %collective-permute-start = (bf16[32,128]{1,0:T(8,128)(2,1)S(1)}, bf16[32,128]{1,0:T(8,128)(2,1)S(1)}, u32[]{:S(2)}, u32[]{:S(2)}) collective-permute-start(bf16[32,128]{1,0:T(8,128)(2,1)S(1)} %get-tuple-element.13.rest_0_), channel_id=1, source_target_pairs={{0,9},{1,8},{2,11},{3,10},{4,13},{5,12},{6,15},{7,14},{8,1},{9,0},... | collective-permute-start | bytes 24584 | tf_op jit(solution)/shard_map/ppermute | solution.py:160
  5.4 0.7 %collective-permute-start.5 = (bf16[16,16,128]{2,1,0:T(8,128)(2,1)S(1)}, bf16[16,16,128]{2,1,0:T(8,128)(2,1)S(1)}, u32[]{:S(2)}, u32[]{:S(2)}) collective-permute-start(bf16[16,16,128]{2,1,0:T(8,128)(2,1)S(1)} %get-tuple-element.15), channel_id=1, source_target_pairs={{0,1},{1,0},{2,3},{3,2},{4,5},{5,4},{6,7},{7,6},{8,9},{9,8},{10,11... | collective-permute-start | bytes 196616 | tf_op jit(solution)/shard_map/ppermute | solution.py:160
  6.0 0.0 slice-start
  6.0 0.0 copy-start.3
  6.0 0.0 copy-start.4
  6.0 0.0 slice-start.1
  6.0 0.0 copy-start
  6.1 0.0 copy-start.1
  6.1 0.1 collective-permute-start.6
  6.2 0.6 %collective-permute-done.rest_1_ = bf16[32,128]{1,0:T(8,128)(2,1)S(1)} collective-permute-done((bf16[32,128]{1,0:T(8,128)(2,1)S(1)}, bf16[32,128]{1,0:T(8,128)(2,1)S(1)}, u32[]{:S(2)}, u32[]{:S(2)}) %collective-permute-start) | collective-permute-done | bytes 8224 | tf_op jit(solution)/shard_map/ppermute | solution.py:160
  6.7 3.1 %collective-permute-start.1 = (bf16[64,128]{1,0:T(8,128)(2,1)S(1)}, bf16[64,128]{1,0:T(8,128)(2,1)S(1)}, u32[]{:S(2)}, u32[]{:S(2)}) collective-permute-start(bf16[64,128]{1,0:T(8,128)(2,1)S(1)} %get-tuple-element.18), channel_id=1, source_target_pairs={{0,6},{1,7},{2,4},{3,5},{4,2},{5,3},{6,0},{7,1},{8,14},{9,15},{10,... | collective-permute-start | bytes 49160 | tf_op jit(solution)/shard_map/ppermute | solution.py:160
  9.8 0.0 copy-done.3
  9.8 0.0 copy-done.4
  9.9 0.2 %weights.1 = (f32[2,32,8,128]{3,2,1,0:T(8,128)S(1)}, s32[32,8,128]{2,1,0:T(8,128)S(1)}) custom-call(s32[1,32]{1,0:T(1,128)S(1)} %bitcast.11, f32[2,32]{1,0:T(2,128)S(1)} %copy-done.3, f32[8,128]{1,0:T(8,128)S(1)} %mark.1), custom_call_target="tpu_custom_call" | custom-call | flops 1000000000 | bytes 1000000 | tf_op jit(solution)/shard_map/weights/pallas_call | solution.py:238
  10.0 0.4 %collective-permute-start.3 = (bf16[64,128]{1,0:T(8,128)(2,1)S(1)}, bf16[64,128]{1,0:T(8,128)(2,1)S(1)}, u32[]{:S(2)}, u32[]{:S(2)}) collective-permute-start(bf16[64,128]{1,0:T(8,128)(2,1)S(1)} %get-tuple-element.18), channel_id=1, source_target_pairs={{0,5},{1,4},{2,7},{3,6},{4,1},{5,0},{6,3},{7,2},{8,13},{9,12},{10,... | collective-permute-start | bytes 49160 | tf_op jit(solution)/shard_map/ppermute | solution.py:160
  10.4 0.1 collective-permute-start.2
  10.6 1.1 %collective-permute-done.1.rest_2_ = bf16[64,128]{1,0:T(8,128)(2,1)S(1)} collective-permute-done((bf16[64,128]{1,0:T(8,128)(2,1)S(1)}, bf16[64,128]{1,0:T(8,128)(2,1)S(1)}, u32[]{:S(2)}, u32[]{:S(2)}) %collective-permute-start.1) | collective-permute-done | bytes 16416 | tf_op jit(solution)/shard_map/ppermute | solution.py:160
  11.7 1.9 %collective-permute-done.2.rest_3_ = bf16[64,128]{1,0:T(8,128)(2,1)S(1)} collective-permute-done((bf16[64,128]{1,0:T(8,128)(2,1)S(1)}, bf16[64,128]{1,0:T(8,128)(2,1)S(1)}, u32[]{:S(2)}, u32[]{:S(2)}) %collective-permute-start.2) | collective-permute-done | bytes 16416 | tf_op jit(solution)/shard_map/ppermute | solution.py:160
  13.6 0.0 collective-permute-done.3.rest_4_
  13.6 0.3 %collective-permute-start.4 = (bf16[256,128]{1,0:T(8,128)(2,1)S(1)}, bf16[256,128]{1,0:T(8,128)(2,1)S(1)}, u32[]{:S(2)}, u32[]{:S(2)}) collective-permute-start(bf16[256,128]{1,0:T(8,128)(2,1)S(1)} %constant_dynamic-update-slice_fusion.2), channel_id=1, source_target_pairs={{0,1},{1,0},{2,3},{3,2},{4,5},{5,4},{6,7},{7,6},{8,9},{9,8},{10,11... | collective-permute-start | bytes 196616 | tf_op jit(solution)/shard_map/ppermute | solution.py:160
  13.9 0.0 collective-permute-done.6.rest_0_
  13.9 0.3 %collective-permute-start.7 = (bf16[16,16,128]{2,1,0:T(8,128)(2,1)S(1)}, bf16[16,16,128]{2,1,0:T(8,128)(2,1)S(1)}, u32[]{:S(2)}, u32[]{:S(2)}) collective-permute-start(bf16[16,16,128]{2,1,0:T(8,128)(2,1)S(1)} %collective-permute-done.6.rest_0_), channel_id=1, source_target_pairs={{0,1},{1,0},{2,3},{3,2},{4,5},{5,4},{6,7},{7,6},{8,9},{9,8},{10,11... | collective-permute-start | bytes 196616 | tf_op jit(solution)/shard_map/ppermute | solution.py:160
  14.2 0.0 collective-permute-done.5.rest_0_
  14.2 0.0 slice-done
  14.2 0.0 slice-done.1
  14.2 0.0 copy-done
  14.2 0.0 copy-done.1
  14.2 1.2 %shard_map.82.rest_6_ = f32[16,16,128]{2,1,0:T(8,128)S(1)} custom-call(s32[8,32]{1,0:T(8,128)S(1)} %bitcast.5, s32[1,32]{1,0:T(1,128)S(1)} %bitcast.8, bf16[32,16,128]{2,1,0:T(8,128)(2,1)S(1)} %get-tuple-element.14.density, bf16[16,16,128]{2,1,0:T(8,128)(2,1)S(1)} %collective-permute-done.5.rest_0_, bf16[32,8,128,128]{3,2,1,0:T(8,128)(2,1)S(1)} %bitcast.4), custom_call_target="tpu_custom_call" | custom-call | flops 2000000000 | bytes 1000000 | tf_op jit(solution)/shard_map/pallas_call | solution.py:257
  15.4 0.0 copy-start.2
  15.4 0.0 collective-permute-done.7.rest_1_
  15.4 0.6 %shard_map.83.rest_7_ = f32[6,16,128]{2,1,0:T(8,128)S(1)} custom-call(s32[8,32]{1,0:T(8,128)S(1)} %bitcast.6, s32[1,32]{1,0:T(1,128)S(1)} %bitcast.9, bf16[32,16,128]{2,1,0:T(8,128)(2,1)S(1)} %get-tuple-element.14.density, bf16[16,16,128]{2,1,0:T(8,128)(2,1)S(1)} %collective-permute-done.6.rest_0_, bf16[16,16,128]{2,1,0:T(8,128)(2,1)S(1)} %collective-permute-done.7.rest_1_, ...), custom_call_target="tpu_custom_call" | custom-call | flops 2000000000 | bytes 1000000 | tf_op jit(solution)/shard_map/pallas_call | solution.py:257
  16.0 0.9 %shard_map.84.rest_8_ = f32[10,16,128]{2,1,0:T(8,128)S(1)} custom-call(s32[8,32]{1,0:T(8,128)S(1)} %bitcast.7, s32[1,32]{1,0:T(1,128)S(1)} %bitcast.10, bf16[32,16,128]{2,1,0:T(8,128)(2,1)S(1)} %get-tuple-element.14.density, bf16[16,16,128]{2,1,0:T(8,128)(2,1)S(1)} %collective-permute-done.6.rest_0_, ...), custom_call_target="tpu_custom_call" | custom-call | flops 2000000000 | bytes 1000000 | tf_op jit(solution)/shard_map/pallas_call | solution.py:257
  16.9 0.0 collective-permute-done.4.rest_5_
  16.9 0.0 copy-done.2
  16.9 1.0 %far.1 = bf16[32,16,128]{2,1,0:T(8,128)(2,1)} custom-call(f32[2,32,8,128]{3,2,1,0:T(8,128)S(1)} %get-tuple-element.11.weights, s32[32,8,128]{2,1,0:T(8,128)S(1)} %get-tuple-element.12.second, bf16[32,128,128]{2,1,0:T(8,128)(2,1)S(1)} %copy-done.2, bf16[32,128]{1,0:T(8,128)(2,1)S(1)} %get-tuple-element.13.rest_0_, ...), custom_call_target="tpu_custom_call" | custom-call | flops 1000000000 | bytes 1000000 | tf_op jit(solution)/shard_map/far/pallas_call | solution.py:259
  (7 shorter events, 0.0 us)
Async XLA Ops:
  1.8 4.9 %collective-permute-start = (bf16[32,128]{1,0:T(8,128)(2,1)S(1)}, bf16[32,128]{1,0:T(8,128)(2,1)S(1)}, u32[]{:S(2)}, u32[]{:S(2)}) collective-permute-start(bf16[32,128]{1,0:T(8,128)(2,1)S(1)} %get-tuple-element.13.rest_0_), channel_id=1, source_target_pairs={{0,9},{1,8},{2,11},{3,10},{4,13},{5,12},{6,15},{7,14},{8,1},{9,0},... | collective-permute-start | bytes 24584 | tf_op jit(solution)/shard_map/ppermute | solution.py:160
  5.4 8.8 %collective-permute-start.5 = (bf16[16,16,128]{2,1,0:T(8,128)(2,1)S(1)}, bf16[16,16,128]{2,1,0:T(8,128)(2,1)S(1)}, u32[]{:S(2)}, u32[]{:S(2)}) collective-permute-start(bf16[16,16,128]{2,1,0:T(8,128)(2,1)S(1)} %get-tuple-element.15), channel_id=1, source_target_pairs={{0,1},{1,0},{2,3},{3,2},{4,5},{5,4},{6,7},{7,6},{8,9},{9,8},{10,11... | collective-permute-start | bytes 196616 | tf_op jit(solution)/shard_map/ppermute | solution.py:160
  6.0 8.1 %slice-start = ((s8[8388608]{0:T(1024)(128)(4,1)}), s8[4194304]{0:T(1024)(128)(4,1)S(1)}, s32[]{:S(2)}) async-start(s8[8388608]{0:T(1024)(128)(4,1)} %bitcast.3), calls=%async_computation | async-start | bytes 8388608
  6.0 3.8 %copy-start.3 = (f32[2,32]{1,0:T(2,128)S(1)}, f32[2,32]{1,0:T(2,128)}, u32[]{:S(2)}) copy-start(f32[2,32]{1,0:T(2,128)} %coupling.1) | copy-start | bytes 772
  6.0 3.8 %copy-start.4 = (s32[32]{0:T(128)S(1)}, s32[32]{0:T(128)}, u32[]{:S(2)}) copy-start(s32[32]{0:T(128)} %coarse_in.1) | copy-start | bytes 388
  6.0 8.1 %slice-start.1 = ((s8[8388608]{0:T(1024)(128)(4,1)}), s8[4194304]{0:T(1024)(128)(4,1)S(1)}, s32[]{:S(2)}) async-start(s8[8388608]{0:T(1024)(128)(4,1)} %bitcast.3), calls=%async_computation.1 | async-start | bytes 8388608
  6.0 8.1 %copy-start = (s32[32,8]{0,1:T(8,128)S(1)}, s32[32,8]{0,1:T(8,128)}, u32[]{:S(2)}) copy-start(s32[32,8]{0,1:T(8,128)} %param.10) | copy-start | bytes 3076
  6.1 8.1 %copy-start.1 = (s32[32]{0:T(128)S(1)}, s32[32]{0:T(128)}, u32[]{:S(2)}) copy-start(s32[32]{0:T(128)} %param.11) | copy-start | bytes 388
  6.1 7.9 %collective-permute-start.6 = (bf16[16,16,128]{2,1,0:T(8,128)(2,1)S(1)}, bf16[16,16,128]{2,1,0:T(8,128)(2,1)S(1)}, u32[]{:S(2)}, u32[]{:S(2)}) collective-permute-start(bf16[16,16,128]{2,1,0:T(8,128)(2,1)S(1)} %get-tuple-element.16), channel_id=1, source_target_pairs={{0,1},{1,2},{2,0},{3,4},{4,3},{5,6},{6,5},{7,8},{8,7},{9,10},{10,9... | collective-permute-start | bytes 196616 | tf_op jit(solution)/shard_map/ppermute | solution.py:214
  6.7 5.0 %collective-permute-start.1 = (bf16[64,128]{1,0:T(8,128)(2,1)S(1)}, bf16[64,128]{1,0:T(8,128)(2,1)S(1)}, u32[]{:S(2)}, u32[]{:S(2)}) collective-permute-start(bf16[64,128]{1,0:T(8,128)(2,1)S(1)} %get-tuple-element.18), channel_id=1, source_target_pairs={{0,6},{1,7},{2,4},{3,5},{4,2},{5,3},{6,0},{7,1},{8,14},{9,15},{10,... | collective-permute-start | bytes 49160 | tf_op jit(solution)/shard_map/ppermute | solution.py:160
  10.0 3.5 %collective-permute-start.3 = (bf16[64,128]{1,0:T(8,128)(2,1)S(1)}, bf16[64,128]{1,0:T(8,128)(2,1)S(1)}, u32[]{:S(2)}, u32[]{:S(2)}) collective-permute-start(bf16[64,128]{1,0:T(8,128)(2,1)S(1)} %get-tuple-element.18), channel_id=1, source_target_pairs={{0,5},{1,4},{2,7},{3,6},{4,1},{5,0},{6,3},{7,2},{8,13},{9,12},{10,... | collective-permute-start | bytes 49160 | tf_op jit(solution)/shard_map/ppermute | solution.py:160
  10.4 3.2 %collective-permute-start.2 = (bf16[64,128]{1,0:T(8,128)(2,1)S(1)}, bf16[64,128]{1,0:T(8,128)(2,1)S(1)}, u32[]{:S(2)}, u32[]{:S(2)}) collective-permute-start(bf16[64,128]{1,0:T(8,128)(2,1)S(1)} %get-tuple-element.18), channel_id=1, source_target_pairs={{0,3},{1,2},{2,1},{3,0},{4,7},{5,6},{6,5},{7,4},{8,11},{9,10},{10,... | collective-permute-start | bytes 49160 | tf_op jit(solution)/shard_map/ppermute | solution.py:160
  13.6 3.3 %collective-permute-start.4 = (bf16[256,128]{1,0:T(8,128)(2,1)S(1)}, bf16[256,128]{1,0:T(8,128)(2,1)S(1)}, u32[]{:S(2)}, u32[]{:S(2)}) collective-permute-start(bf16[256,128]{1,0:T(8,128)(2,1)S(1)} %constant_dynamic-update-slice_fusion.2), channel_id=1, source_target_pairs={{0,1},{1,0},{2,3},{3,2},{4,5},{5,4},{6,7},{7,6},{8,9},{9,8},{10,11... | collective-permute-start | bytes 196616 | tf_op jit(solution)/shard_map/ppermute | solution.py:160
  13.9 1.5 %collective-permute-start.7 = (bf16[16,16,128]{2,1,0:T(8,128)(2,1)S(1)}, bf16[16,16,128]{2,1,0:T(8,128)(2,1)S(1)}, u32[]{:S(2)}, u32[]{:S(2)}) collective-permute-start(bf16[16,16,128]{2,1,0:T(8,128)(2,1)S(1)} %collective-permute-done.6.rest_0_), channel_id=1, source_target_pairs={{0,1},{1,0},{2,3},{3,2},{4,5},{5,4},{6,7},{7,6},{8,9},{9,8},{10,11... | collective-permute-start | bytes 196616 | tf_op jit(solution)/shard_map/ppermute | solution.py:160
  15.4 1.5 %copy-start.2 = (bf16[32,128,128]{2,1,0:T(8,128)(2,1)S(1)}, bf16[32,128,128]{2,1,0:T(8,128)(2,1)}, u32[]{:S(2)}) copy-start(bf16[32,128,128]{2,1,0:T(8,128)(2,1)} %evaluate.1) | copy-start | bytes 3145732

commit v4 on v3

--- a/solution.py
+++ b/solution.py
@@ -43,14 +43,10 @@
             here = (coarse[b] - first) == c
             rows, lanes = slice(c * columns, (c + 1) * columns), slice(b * panels, (b + 1) * panels)
             masked[rows, lanes] = jnp.where(here, block, jnp.zeros_like(block))
-    total = None
-    for i in range(chunks):
-        copies[2 + i].wait()
-        right = jnp.concatenate([restrict[b] for b in range(i * size, (i + 1) * size)], axis=1)
-        left = masked[:, i * size * panels : (i + 1) * size * panels]
-        part = lax.dot_general(left, right, NT, preferred_element_type=F32)
-        total = part if total is None else total + part
-    out[...] = total.astype(out.dtype)
+    for copy in copies[2:]:
+        copy.wait()
+    right = jnp.concatenate([restrict[b] for b in range(blk_count)], axis=1)
+    out[...] = lax.dot_general(masked[...], right, NT, preferred_element_type=F32).astype(out.dtype)
 
 
 def near_kernel(on, begin, ids, counts, density, *rest):
@@ -112,15 +108,16 @@
     groups, _ = weights.shape[:2]
     local = []
     for c in range(groups):
-        total = jnp.zeros((columns, panels), F32)
-        s = 0
+        terms = []
         for piece in moments:
             for at in range(0, piece.shape[0], columns):
                 row = piece[pl.ds(at, columns)].astype(F32)
-                weight = weights[c, s]
-                total += row * jnp.concatenate([weight] * (columns // weight.shape[0]), axis=0)
-                s += 1
-        local.append(total.astype(BF16))
+                weight = weights[c, len(terms)]
+                terms.append(row * jnp.concatenate([weight] * (columns // weight.shape[0]), axis=0))
+        while len(terms) > 1:
+            half_terms = len(terms) // 2
+            terms = [terms[i] + terms[i + half_terms] for i in range(half_terms)] + terms[2 * half_terms :]
+        local.append(terms[0].astype(BF16))
     left = jnp.concatenate(local, axis=0)
     half = blk_count // 2
     odd = lax.rem(lax.axis_index("panel"), 2)
@@ -182,7 +179,7 @@
         masks = masks + [mask ^ step for step in together for mask in masks]
 
     half_shape = (half, columns, panels)
-    chunks = 1
+    chunks = 4
     moments, kept, to_chip, to_off = pl.pallas_call(
         functools.partial(moments_kernel, chunks),
         out_shape=(
@@ -267,11 +264,11 @@
     )(*on_chip(weights, second, evaluate, *pieces, *near))
 
 
-CUTS = ((True, 0, 8), (False, 0, 3), (False, 3, 8))
+CUTS = ((True, 0, 8), (False, 0, 4), (False, 4, 8))
 
 
 def rounds_of(count):
-    return [[(1 << bit) | 1] for bit in range(count.bit_length() - 2, 2, -1)] + [[6, 3, 5], [1]]
+    return [[(1 << bit) | 1] for bit in range(count.bit_length() - 2, 2, -1)] + [[7, 5, 3], [1]]
 
 
 def solution(mesh):

time: 18.1 us -> 18.1 us (level)
  starting transfers between devices: 8.5 us -> 8.98 us
  waiting for transfers between devices: 3.61 us -> 3.15 us
    ppermute x7, starting transfers between devices: 8.43 us -> 8.91 us  [exchange(): return lax.ppermute(x, 'panel', [(i, i ^ step) for i in range(count)])]
    ppermute x7, waiting for transfers between devices: 3.6 us -> 3.15 us  [exchange(): return lax.ppermute(x, 'panel', [(i, i ^ step) for i in range(count)])]
where the time goes in v4:
time: 18.1 us; the launch traced here: 17.9 us
  starting transfers between devices  8.98 us (50%)
  Pallas kernels  5.62 us (31%)
  waiting for transfers between devices  3.15 us (17%)
    ppermute x7, starting transfers between devices, exchange(): return lax.ppermute(x, 'panel', [(i, i ^ step) for i in range(count)])  8.91 us
    ppermute x7, waiting for transfers between devices, exchange(): return lax.ppermute(x, 'panel', [(i, i ^ step) for i in range(count)])  3.15 us
    pallas_call x3, Pallas kernels, body(): near.append(call(*on_chip(ids, live_counts, kept, *halos, near_blocks)))  2.68 us
    pallas_call x1, Pallas kernels, body(): pl.pallas_call(functools.partial(moments_kernel, chunks), out_shape=(pltp...  1.76 us
    pallas_call x1, Pallas kernels, body(): pl.pallas_call(functools.partial(far_kernel, cuts, len(pieces)), out_shap...  0.98 us
  transfers between devices with their start and end apart: 8, of which 3 were waited for; matrix products, arithmetic and copies ran while one was open for 0% of the time, Pallas kernels for 16%

profile of v4, /device:TPU:0, one launch (start us, length us, event | category | flops | bytes accessed | tf_op | source)
XLA Modules:
  0.0 17.9 jit_solution(12394268352581070716)
XLA Ops:
  0.0 1.8 %moments.1 = (bf16[32,128]{1,0:T(8,128)(2,1)S(1)}, bf16[32,16,128]{2,1,0:T(8,128)(2,1)S(1)}, bf16[16,16,128]{2,1,0:T(8,128)(2,1)S(1)}, bf16[16,16,128]{2,1,0:T(8,128)(2,1)S(1)}) custom-call(s32[32]{0:T(128)} %coarse_in.1, bf16[32,16,128]{2,1,0:T(8,128)(2,1)} %density_in.1, bf16[32,128,128]{2,1,0:T(8,128)(2,1)} %restrict_in.1), custom_call_target="tpu_custom_call" | custom-call | flops 10000000000 | bytes 1000000 | tf_op jit(solution)/shard_map/moments/pallas_call | solution.py:183
  1.8 3.6 %collective-permute-start = (bf16[32,128]{1,0:T(8,128)(2,1)S(1)}, bf16[32,128]{1,0:T(8,128)(2,1)S(1)}, u32[]{:S(2)}, u32[]{:S(2)}) collective-permute-start(bf16[32,128]{1,0:T(8,128)(2,1)S(1)} %get-tuple-element.13.rest_0_), channel_id=1, source_target_pairs={{0,9},{1,8},{2,11},{3,10},{4,13},{5,12},{6,15},{7,14},{8,1},{9,0},... | collective-permute-start | bytes 24584 | tf_op jit(solution)/shard_map/ppermute | solution.py:157
  5.3 0.7 %collective-permute-start.5 = (bf16[16,16,128]{2,1,0:T(8,128)(2,1)S(1)}, bf16[16,16,128]{2,1,0:T(8,128)(2,1)S(1)}, u32[]{:S(2)}, u32[]{:S(2)}) collective-permute-start(bf16[16,16,128]{2,1,0:T(8,128)(2,1)S(1)} %get-tuple-element.15), channel_id=1, source_target_pairs={{0,1},{1,0},{2,3},{3,2},{4,5},{5,4},{6,7},{7,6},{8,9},{9,8},{10,11... | collective-permute-start | bytes 196616 | tf_op jit(solution)/shard_map/ppermute | solution.py:157
  6.0 0.0 slice-start
  6.0 0.0 copy-start.3
  6.0 0.0 copy-start.4
  6.0 0.0 slice-start.1
  6.0 0.0 copy-start
  6.0 0.0 copy-start.1
  6.0 0.1 collective-permute-start.6
  6.1 0.6 %collective-permute-done.rest_1_ = bf16[32,128]{1,0:T(8,128)(2,1)S(1)} collective-permute-done((bf16[32,128]{1,0:T(8,128)(2,1)S(1)}, bf16[32,128]{1,0:T(8,128)(2,1)S(1)}, u32[]{:S(2)}, u32[]{:S(2)}) %collective-permute-start) | collective-permute-done | bytes 8224 | tf_op jit(solution)/shard_map/ppermute | solution.py:157
  6.7 2.8 %collective-permute-start.1 = (bf16[64,128]{1,0:T(8,128)(2,1)S(1)}, bf16[64,128]{1,0:T(8,128)(2,1)S(1)}, u32[]{:S(2)}, u32[]{:S(2)}) collective-permute-start(bf16[64,128]{1,0:T(8,128)(2,1)S(1)} %get-tuple-element.18), channel_id=1, source_target_pairs={{0,7},{1,6},{2,5},{3,4},{4,3},{5,2},{6,1},{7,0},{8,15},{9,14},{10,... | collective-permute-start | bytes 49160 | tf_op jit(solution)/shard_map/ppermute | solution.py:157
  9.5 0.0 copy-done.3
  9.5 0.0 copy-done.4
  9.5 0.2 %weights.1 = (f32[2,32,8,128]{3,2,1,0:T(8,128)S(1)}, s32[32,8,128]{2,1,0:T(8,128)S(1)}) custom-call(s32[1,32]{1,0:T(1,128)S(1)} %bitcast.11, f32[2,32]{1,0:T(2,128)S(1)} %copy-done.3, f32[8,128]{1,0:T(8,128)S(1)} %mark.1), custom_call_target="tpu_custom_call" | custom-call | flops 1000000000 | bytes 1000000 | tf_op jit(solution)/shard_map/weights/pallas_call | solution.py:235
  9.7 0.6 %collective-permute-start.3 = (bf16[64,128]{1,0:T(8,128)(2,1)S(1)}, bf16[64,128]{1,0:T(8,128)(2,1)S(1)}, u32[]{:S(2)}, u32[]{:S(2)}) collective-permute-start(bf16[64,128]{1,0:T(8,128)(2,1)S(1)} %get-tuple-element.18), channel_id=1, source_target_pairs={{0,3},{1,2},{2,1},{3,0},{4,7},{5,6},{6,5},{7,4},{8,11},{9,10},{10,... | collective-permute-start | bytes 49160 | tf_op jit(solution)/shard_map/ppermute | solution.py:157
  10.3 0.6 %collective-permute-start.2 = (bf16[64,128]{1,0:T(8,128)(2,1)S(1)}, bf16[64,128]{1,0:T(8,128)(2,1)S(1)}, u32[]{:S(2)}, u32[]{:S(2)}) collective-permute-start(bf16[64,128]{1,0:T(8,128)(2,1)S(1)} %get-tuple-element.18), channel_id=1, source_target_pairs={{0,5},{1,4},{2,7},{3,6},{4,1},{5,0},{6,3},{7,2},{8,13},{9,12},{10,... | collective-permute-start | bytes 49160 | tf_op jit(solution)/shard_map/ppermute | solution.py:157
  10.9 0.1 collective-permute-done.1.rest_2_
  11.0 2.5 %collective-permute-done.2.rest_3_ = bf16[64,128]{1,0:T(8,128)(2,1)S(1)} collective-permute-done((bf16[64,128]{1,0:T(8,128)(2,1)S(1)}, bf16[64,128]{1,0:T(8,128)(2,1)S(1)}, u32[]{:S(2)}, u32[]{:S(2)}) %collective-permute-start.2) | collective-permute-done | bytes 16416 | tf_op jit(solution)/shard_map/ppermute | solution.py:157
  13.5 0.0 collective-permute-done.3.rest_4_
  13.5 0.6 %collective-permute-start.4 = (bf16[256,128]{1,0:T(8,128)(2,1)S(1)}, bf16[256,128]{1,0:T(8,128)(2,1)S(1)}, u32[]{:S(2)}, u32[]{:S(2)}) collective-permute-start(bf16[256,128]{1,0:T(8,128)(2,1)S(1)} %constant_dynamic-update-slice_fusion.2), channel_id=1, source_target_pairs={{0,1},{1,0},{2,3},{3,2},{4,5},{5,4},{6,7},{7,6},{8,9},{9,8},{10,11... | collective-permute-start | bytes 196616 | tf_op jit(solution)/shard_map/ppermute | solution.py:157
  14.1 0.0 collective-permute-done.6.rest_0_
  14.1 0.1 collective-permute-start.7
  14.2 0.0 collective-permute-done.5.rest_0_
  14.2 0.0 slice-done
  14.2 0.0 slice-done.1
  14.2 0.0 copy-done
  14.2 0.0 copy-done.1
  14.2 1.2 %shard_map.82.rest_6_ = f32[16,16,128]{2,1,0:T(8,128)S(1)} custom-call(s32[8,32]{1,0:T(8,128)S(1)} %bitcast.5, s32[1,32]{1,0:T(1,128)S(1)} %bitcast.8, bf16[32,16,128]{2,1,0:T(8,128)(2,1)S(1)} %get-tuple-element.14.density, bf16[16,16,128]{2,1,0:T(8,128)(2,1)S(1)} %collective-permute-done.5.rest_0_, bf16[32,8,128,128]{3,2,1,0:T(8,128)(2,1)S(1)} %bitcast.4), custom_call_target="tpu_custom_call" | custom-call | flops 2000000000 | bytes 1000000 | tf_op jit(solution)/shard_map/pallas_call | solution.py:254
  15.4 0.0 copy-start.2
  15.4 0.0 collective-permute-done.7.rest_1_
  15.4 0.7 %shard_map.84.rest_8_ = f32[8,16,128]{2,1,0:T(8,128)S(1)} custom-call(s32[8,32]{1,0:T(8,128)S(1)} %bitcast.6, s32[1,32]{1,0:T(1,128)S(1)} %bitcast.9, bf16[32,16,128]{2,1,0:T(8,128)(2,1)S(1)} %get-tuple-element.14.density, bf16[16,16,128]{2,1,0:T(8,128)(2,1)S(1)} %collective-permute-done.6.rest_0_, bf16[16,16,128]{2,1,0:T(8,128)(2,1)S(1)} %collective-permute-done.7.rest_1_, ...), custom_call_target="tpu_custom_call" | custom-call | flops 2000000000 | bytes 1000000 | tf_op jit(solution)/shard_map/pallas_call | solution.py:254
  16.2 0.8 %shard_map.83.rest_7_ = f32[8,16,128]{2,1,0:T(8,128)S(1)} custom-call(s32[8,32]{1,0:T(8,128)S(1)} %bitcast.7, s32[1,32]{1,0:T(1,128)S(1)} %bitcast.10, bf16[32,16,128]{2,1,0:T(8,128)(2,1)S(1)} %get-tuple-element.14.density, bf16[16,16,128]{2,1,0:T(8,128)(2,1)S(1)} %collective-permute-done.6.rest_0_, bf16[16,16,128]{2,1,0:T(8,128)(2,1)S(1)} %collective-permute-done.7.rest_1_, ...), custom_call_target="tpu_custom_call" | custom-call | flops 2000000000 | bytes 1000000 | tf_op jit(solution)/shard_map/pallas_call | solution.py:254
  16.9 0.0 collective-permute-done.4.rest_5_
  16.9 0.0 copy-done.2
  16.9 1.0 %far.1 = bf16[32,16,128]{2,1,0:T(8,128)(2,1)} custom-call(f32[2,32,8,128]{3,2,1,0:T(8,128)S(1)} %get-tuple-element.11.weights, s32[32,8,128]{2,1,0:T(8,128)S(1)} %get-tuple-element.12.second, bf16[32,128,128]{2,1,0:T(8,128)(2,1)S(1)} %copy-done.2, bf16[32,128]{1,0:T(8,128)(2,1)S(1)} %get-tuple-element.13.rest_0_, ...), custom_call_target="tpu_custom_call" | custom-call | flops 1000000000 | bytes 1000000 | tf_op jit(solution)/shard_map/far/pallas_call | solution.py:256
  (7 shorter events, 0.0 us)
Async XLA Ops:
  1.8 4.9 %collective-permute-start = (bf16[32,128]{1,0:T(8,128)(2,1)S(1)}, bf16[32,128]{1,0:T(8,128)(2,1)S(1)}, u32[]{:S(2)}, u32[]{:S(2)}) collective-permute-start(bf16[32,128]{1,0:T(8,128)(2,1)S(1)} %get-tuple-element.13.rest_0_), channel_id=1, source_target_pairs={{0,9},{1,8},{2,11},{3,10},{4,13},{5,12},{6,15},{7,14},{8,1},{9,0},... | collective-permute-start | bytes 24584 | tf_op jit(solution)/shard_map/ppermute | solution.py:157
  5.3 8.8 %collective-permute-start.5 = (bf16[16,16,128]{2,1,0:T(8,128)(2,1)S(1)}, bf16[16,16,128]{2,1,0:T(8,128)(2,1)S(1)}, u32[]{:S(2)}, u32[]{:S(2)}) collective-permute-start(bf16[16,16,128]{2,1,0:T(8,128)(2,1)S(1)} %get-tuple-element.15), channel_id=1, source_target_pairs={{0,1},{1,0},{2,3},{3,2},{4,5},{5,4},{6,7},{7,6},{8,9},{9,8},{10,11... | collective-permute-start | bytes 196616 | tf_op jit(solution)/shard_map/ppermute | solution.py:157
  6.0 8.2 %slice-start = ((s8[8388608]{0:T(1024)(128)(4,1)}), s8[4194304]{0:T(1024)(128)(4,1)S(1)}, s32[]{:S(2)}) async-start(s8[8388608]{0:T(1024)(128)(4,1)} %bitcast.3), calls=%async_computation | async-start | bytes 8388608
  6.0 3.5 %copy-start.3 = (f32[2,32]{1,0:T(2,128)S(1)}, f32[2,32]{1,0:T(2,128)}, u32[]{:S(2)}) copy-start(f32[2,32]{1,0:T(2,128)} %coupling.1) | copy-start | bytes 772
  6.0 3.5 %copy-start.4 = (s32[32]{0:T(128)S(1)}, s32[32]{0:T(128)}, u32[]{:S(2)}) copy-start(s32[32]{0:T(128)} %coarse_in.1) | copy-start | bytes 388
  6.0 8.2 %slice-start.1 = ((s8[8388608]{0:T(1024)(128)(4,1)}), s8[4194304]{0:T(1024)(128)(4,1)S(1)}, s32[]{:S(2)}) async-start(s8[8388608]{0:T(1024)(128)(4,1)} %bitcast.3), calls=%async_computation.1 | async-start | bytes 8388608
  6.0 8.2 %copy-start = (s32[32,8]{0,1:T(8,128)S(1)}, s32[32,8]{0,1:T(8,128)}, u32[]{:S(2)}) copy-start(s32[32,8]{0,1:T(8,128)} %param.10) | copy-start | bytes 3076
  6.0 8.2 %copy-start.1 = (s32[32]{0:T(128)S(1)}, s32[32]{0:T(128)}, u32[]{:S(2)}) copy-start(s32[32]{0:T(128)} %param.11) | copy-start | bytes 388
  6.0 8.0 %collective-permute-start.6 = (bf16[16,16,128]{2,1,0:T(8,128)(2,1)S(1)}, bf16[16,16,128]{2,1,0:T(8,128)(2,1)S(1)}, u32[]{:S(2)}, u32[]{:S(2)}) collective-permute-start(bf16[16,16,128]{2,1,0:T(8,128)(2,1)S(1)} %get-tuple-element.16), channel_id=1, source_target_pairs={{0,1},{1,2},{2,0},{3,4},{4,3},{5,6},{6,5},{7,8},{8,7},{9,10},{10,9... | collective-permute-start | bytes 196616 | tf_op jit(solution)/shard_map/ppermute | solution.py:211
  6.7 4.3 %collective-permute-start.1 = (bf16[64,128]{1,0:T(8,128)(2,1)S(1)}, bf16[64,128]{1,0:T(8,128)(2,1)S(1)}, u32[]{:S(2)}, u32[]{:S(2)}) collective-permute-start(bf16[64,128]{1,0:T(8,128)(2,1)S(1)} %get-tuple-element.18), channel_id=1, source_target_pairs={{0,7},{1,6},{2,5},{3,4},{4,3},{5,2},{6,1},{7,0},{8,15},{9,14},{10,... | collective-permute-start | bytes 49160 | tf_op jit(solution)/shard_map/ppermute | solution.py:157
  9.7 3.7 %collective-permute-start.3 = (bf16[64,128]{1,0:T(8,128)(2,1)S(1)}, bf16[64,128]{1,0:T(8,128)(2,1)S(1)}, u32[]{:S(2)}, u32[]{:S(2)}) collective-permute-start(bf16[64,128]{1,0:T(8,128)(2,1)S(1)} %get-tuple-element.18), channel_id=1, source_target_pairs={{0,3},{1,2},{2,1},{3,0},{4,7},{5,6},{6,5},{7,4},{8,11},{9,10},{10,... | collective-permute-start | bytes 49160 | tf_op jit(solution)/shard_map/ppermute | solution.py:157
  10.3 3.2 %collective-permute-start.2 = (bf16[64,128]{1,0:T(8,128)(2,1)S(1)}, bf16[64,128]{1,0:T(8,128)(2,1)S(1)}, u32[]{:S(2)}, u32[]{:S(2)}) collective-permute-start(bf16[64,128]{1,0:T(8,128)(2,1)S(1)} %get-tuple-element.18), channel_id=1, source_target_pairs={{0,5},{1,4},{2,7},{3,6},{4,1},{5,0},{6,3},{7,2},{8,13},{9,12},{10,... | collective-permute-start | bytes 49160 | tf_op jit(solution)/shard_map/ppermute | solution.py:157
  13.5 3.4 %collective-permute-start.4 = (bf16[256,128]{1,0:T(8,128)(2,1)S(1)}, bf16[256,128]{1,0:T(8,128)(2,1)S(1)}, u32[]{:S(2)}, u32[]{:S(2)}) collective-permute-start(bf16[256,128]{1,0:T(8,128)(2,1)S(1)} %constant_dynamic-update-slice_fusion.2), channel_id=1, source_target_pairs={{0,1},{1,0},{2,3},{3,2},{4,5},{5,4},{6,7},{7,6},{8,9},{9,8},{10,11... | collective-permute-start | bytes 196616 | tf_op jit(solution)/shard_map/ppermute | solution.py:157
  14.1 1.3 %collective-permute-start.7 = (bf16[16,16,128]{2,1,0:T(8,128)(2,1)S(1)}, bf16[16,16,128]{2,1,0:T(8,128)(2,1)S(1)}, u32[]{:S(2)}, u32[]{:S(2)}) collective-permute-start(bf16[16,16,128]{2,1,0:T(8,128)(2,1)S(1)} %collective-permute-done.6.rest_0_), channel_id=1, source_target_pairs={{0,1},{1,0},{2,3},{3,2},{4,5},{5,4},{6,7},{7,6},{8,9},{9,8},{10,11... | collective-permute-start | bytes 196616 | tf_op jit(solution)/shard_map/ppermute | solution.py:157
  15.4 1.5 %copy-start.2 = (bf16[32,128,128]{2,1,0:T(8,128)(2,1)S(1)}, bf16[32,128,128]{2,1,0:T(8,128)(2,1)}, u32[]{:S(2)}) copy-start(bf16[32,128,128]{2,1,0:T(8,128)(2,1)} %evaluate.1) | copy-start | bytes 3145732

commit v5 on v4

--- a/solution.py
+++ b/solution.py
@@ -102,22 +102,33 @@
     out[...] = jnp.zeros_like(out)
 
 
-def far_kernel(cuts, parts, weights, second, evaluate, *rest):
-    moments, near, out = rest[:parts], rest[parts:-1], rest[-1]
+def coupled(pieces, weights, c, first, columns):
+    terms = []
+    for piece in pieces:
+        for at in range(0, piece.shape[0], columns):
+            row = piece[pl.ds(at, columns)].astype(F32)
+            weight = weights[c, first + len(terms)]
+            terms.append(row * jnp.concatenate([weight] * (columns // weight.shape[0]), axis=0))
+    while len(terms) > 1:
+        half = len(terms) // 2
+        terms = [terms[i] + terms[i + half] for i in range(half)] + terms[2 * half :]
+    return terms[0]
+
+
+def partial_kernel(weights, *rest):
+    pieces, out = rest[:-1], rest[-1]
+    for c in range(out.shape[0]):
+        out[c] = coupled(pieces, weights, c, 0, out.shape[1])
+
+
+def far_kernel(cuts, weights, second, evaluate, known, last, *rest):
+    near, out = rest[:-1], rest[-1]
     blk_count, columns, panels = out.shape
-    groups, _ = weights.shape[:2]
+    groups, slots = weights.shape[:2]
     local = []
     for c in range(groups):
-        terms = []
-        for piece in moments:
-            for at in range(0, piece.shape[0], columns):
-                row = piece[pl.ds(at, columns)].astype(F32)
-                weight = weights[c, len(terms)]
-                terms.append(row * jnp.concatenate([weight] * (columns // weight.shape[0]), axis=0))
-        while len(terms) > 1:
-            half_terms = len(terms) // 2
-            terms = [terms[i] + terms[i + half_terms] for i in range(half_terms)] + terms[2 * half_terms :]
-        local.append(terms[0].astype(BF16))
+        total = known[c] + coupled((last,), weights, c, slots - last.shape[0] // columns, columns)
+        local.append(total.astype(BF16))
     left = jnp.concatenate(local, axis=0)
     half = blk_count // 2
     odd = lax.rem(lax.axis_index("panel"), 2)
@@ -253,15 +264,26 @@
         )
         near.append(call(*on_chip(ids, live_counts, kept, *halos, near_blocks)))
 
+    make_partial = pl.pallas_call(
+        partial_kernel,
+        out_shape=pltpu.VMEM((groups, columns, panels), F32),
+        in_specs=[VMEM] * len(pieces),
+        out_specs=VMEM,
+        compiler_params=room(4),
+        cost_estimate=cost(10**9, 10**6),
+        name="partial",
+    )
+    known = make_partial(*on_chip(weights, *pieces[:-1]))
+
     return pl.pallas_call(
-        functools.partial(far_kernel, cuts, len(pieces)),
+        functools.partial(far_kernel, cuts),
         out_shape=jax.ShapeDtypeStruct(density.shape, BF16),
-        in_specs=[VMEM] * (3 + len(pieces) + len(near)),
+        in_specs=[VMEM] * (5 + len(near)),
         out_specs=VMEM,
         compiler_params=room(4),
         cost_estimate=cost(10**9, 10**6),
         name="far",
-    )(*on_chip(weights, second, evaluate, *pieces, *near))
+    )(*on_chip(weights, second, evaluate, known, pieces[-1], *near))
 
 
 CUTS = ((True, 0, 8), (False, 0, 4), (False, 4, 8))

time: 18.1 us -> 18.1 us (level)
    pallas_call x1 -> x2, Pallas kernels: 0.98 us -> 0.99 us  [the longest x1 0.95 us: body(): pl.pallas_call(functools.partial(far_kernel, cuts), out_shape=jax.ShapeDt...]
where the time goes in v5:
time: 18.1 us; the launch traced here: 18 us
  starting transfers between devices  8.98 us (50%)
  Pallas kernels  5.63 us (31%)
  waiting for transfers between devices  3.15 us (17%)
    ppermute x7, starting transfers between devices, exchange(): return lax.ppermute(x, 'panel', [(i, i ^ step) for i in range(count)])  8.91 us
    ppermute x7, waiting for transfers between devices, exchange(): return lax.ppermute(x, 'panel', [(i, i ^ step) for i in range(count)])  3.15 us
    pallas_call x3, Pallas kernels, body(): near.append(call(*on_chip(ids, live_counts, kept, *halos, near_blocks)))  2.68 us
    pallas_call x1, Pallas kernels, body(): pl.pallas_call(functools.partial(moments_kernel, chunks), out_shape=(pltp...  1.76 us
    pallas_call x1, Pallas kernels, body(): pl.pallas_call(functools.partial(far_kernel, cuts), out_shape=jax.ShapeDt...  0.95 us
  transfers between devices with their start and end apart: 8, of which 3 were waited for; matrix products, arithmetic and copies ran while one was open for 0% of the time, Pallas kernels for 16%

profile of v5, /device:TPU:0, one launch (start us, length us, event | category | flops | bytes accessed | tf_op | source)
XLA Modules:
  0.0 18.0 jit_solution(3755727850500260194)
XLA Ops:
  0.0 1.8 %moments.1 = (bf16[32,128]{1,0:T(8,128)(2,1)S(1)}, bf16[32,16,128]{2,1,0:T(8,128)(2,1)S(1)}, bf16[16,16,128]{2,1,0:T(8,128)(2,1)S(1)}, bf16[16,16,128]{2,1,0:T(8,128)(2,1)S(1)}) custom-call(s32[32]{0:T(128)} %coarse_in.1, bf16[32,16,128]{2,1,0:T(8,128)(2,1)} %density_in.1, bf16[32,128,128]{2,1,0:T(8,128)(2,1)} %restrict_in.1), custom_call_target="tpu_custom_call" | custom-call | flops 10000000000 | bytes 1000000 | tf_op jit(solution)/shard_map/moments/pallas_call | solution.py:194
  1.8 3.6 %collective-permute-start = (bf16[32,128]{1,0:T(8,128)(2,1)S(1)}, bf16[32,128]{1,0:T(8,128)(2,1)S(1)}, u32[]{:S(2)}, u32[]{:S(2)}) collective-permute-start(bf16[32,128]{1,0:T(8,128)(2,1)S(1)} %get-tuple-element.13.rest_0_), channel_id=1, source_target_pairs={{0,9},{1,8},{2,11},{3,10},{4,13},{5,12},{6,15},{7,14},{8,1},{9,0},... | collective-permute-start | bytes 24584 | tf_op jit(solution)/shard_map/ppermute | solution.py:168
  5.3 0.7 %collective-permute-start.5 = (bf16[16,16,128]{2,1,0:T(8,128)(2,1)S(1)}, bf16[16,16,128]{2,1,0:T(8,128)(2,1)S(1)}, u32[]{:S(2)}, u32[]{:S(2)}) collective-permute-start(bf16[16,16,128]{2,1,0:T(8,128)(2,1)S(1)} %get-tuple-element.15), channel_id=1, source_target_pairs={{0,1},{1,0},{2,3},{3,2},{4,5},{5,4},{6,7},{7,6},{8,9},{9,8},{10,11... | collective-permute-start | bytes 196616 | tf_op jit(solution)/shard_map/ppermute | solution.py:168
  6.0 0.0 slice-start
  6.0 0.0 copy-start.3
  6.0 0.0 copy-start.4
  6.0 0.0 slice-start.1
  6.0 0.0 copy-start
  6.0 0.0 copy-start.1
  6.0 0.1 collective-permute-start.6
  6.1 0.6 %collective-permute-done.rest_1_ = bf16[32,128]{1,0:T(8,128)(2,1)S(1)} collective-permute-done((bf16[32,128]{1,0:T(8,128)(2,1)S(1)}, bf16[32,128]{1,0:T(8,128)(2,1)S(1)}, u32[]{:S(2)}, u32[]{:S(2)}) %collective-permute-start) | collective-permute-done | bytes 8224 | tf_op jit(solution)/shard_map/ppermute | solution.py:168
  6.7 2.8 %collective-permute-start.1 = (bf16[64,128]{1,0:T(8,128)(2,1)S(1)}, bf16[64,128]{1,0:T(8,128)(2,1)S(1)}, u32[]{:S(2)}, u32[]{:S(2)}) collective-permute-start(bf16[64,128]{1,0:T(8,128)(2,1)S(1)} %get-tuple-element.18), channel_id=1, source_target_pairs={{0,7},{1,6},{2,5},{3,4},{4,3},{5,2},{6,1},{7,0},{8,15},{9,14},{10,... | collective-permute-start | bytes 49160 | tf_op jit(solution)/shard_map/ppermute | solution.py:168
  9.5 0.0 copy-done.3
  9.5 0.0 copy-done.4
  9.5 0.2 %weights.1 = (f32[2,32,8,128]{3,2,1,0:T(8,128)S(1)}, s32[32,8,128]{2,1,0:T(8,128)S(1)}) custom-call(s32[1,32]{1,0:T(1,128)S(1)} %bitcast.11, f32[2,32]{1,0:T(2,128)S(1)} %copy-done.3, f32[8,128]{1,0:T(8,128)S(1)} %mark.1), custom_call_target="tpu_custom_call" | custom-call | flops 1000000000 | bytes 1000000 | tf_op jit(solution)/shard_map/weights/pallas_call | solution.py:246
  9.7 0.6 %collective-permute-start.3 = (bf16[64,128]{1,0:T(8,128)(2,1)S(1)}, bf16[64,128]{1,0:T(8,128)(2,1)S(1)}, u32[]{:S(2)}, u32[]{:S(2)}) collective-permute-start(bf16[64,128]{1,0:T(8,128)(2,1)S(1)} %get-tuple-element.18), channel_id=1, source_target_pairs={{0,3},{1,2},{2,1},{3,0},{4,7},{5,6},{6,5},{7,4},{8,11},{9,10},{10,... | collective-permute-start | bytes 49160 | tf_op jit(solution)/shard_map/ppermute | solution.py:168
  10.3 0.6 %collective-permute-start.2 = (bf16[64,128]{1,0:T(8,128)(2,1)S(1)}, bf16[64,128]{1,0:T(8,128)(2,1)S(1)}, u32[]{:S(2)}, u32[]{:S(2)}) collective-permute-start(bf16[64,128]{1,0:T(8,128)(2,1)S(1)} %get-tuple-element.18), channel_id=1, source_target_pairs={{0,5},{1,4},{2,7},{3,6},{4,1},{5,0},{6,3},{7,2},{8,13},{9,12},{10,... | collective-permute-start | bytes 49160 | tf_op jit(solution)/shard_map/ppermute | solution.py:168
  10.9 0.1 collective-permute-done.1.rest_2_
  11.0 2.5 %collective-permute-done.2.rest_3_ = bf16[64,128]{1,0:T(8,128)(2,1)S(1)} collective-permute-done((bf16[64,128]{1,0:T(8,128)(2,1)S(1)}, bf16[64,128]{1,0:T(8,128)(2,1)S(1)}, u32[]{:S(2)}, u32[]{:S(2)}) %collective-permute-start.2) | collective-permute-done | bytes 16416 | tf_op jit(solution)/shard_map/ppermute | solution.py:168
  13.5 0.0 collective-permute-done.3.rest_4_
  13.5 0.6 %collective-permute-start.4 = (bf16[256,128]{1,0:T(8,128)(2,1)S(1)}, bf16[256,128]{1,0:T(8,128)(2,1)S(1)}, u32[]{:S(2)}, u32[]{:S(2)}) collective-permute-start(bf16[256,128]{1,0:T(8,128)(2,1)S(1)} %constant_dynamic-update-slice_fusion.2), channel_id=1, source_target_pairs={{0,1},{1,0},{2,3},{3,2},{4,5},{5,4},{6,7},{7,6},{8,9},{9,8},{10,11... | collective-permute-start | bytes 196616 | tf_op jit(solution)/shard_map/ppermute | solution.py:168
  14.1 0.0 collective-permute-done.6.rest_0_
  14.1 0.1 collective-permute-start.7
  14.2 0.0 collective-permute-done.5.rest_0_
  14.2 0.0 slice-done
  14.2 0.0 slice-done.1
  14.2 0.0 copy-done
  14.3 0.0 copy-done.1
  14.3 1.2 %shard_map.82.rest_0_ = f32[16,16,128]{2,1,0:T(8,128)S(1)} custom-call(s32[8,32]{1,0:T(8,128)S(1)} %bitcast.5, s32[1,32]{1,0:T(1,128)S(1)} %bitcast.8, bf16[32,16,128]{2,1,0:T(8,128)(2,1)S(1)} %get-tuple-element.14.density, bf16[16,16,128]{2,1,0:T(8,128)(2,1)S(1)} %collective-permute-done.5.rest_0_, bf16[32,8,128,128]{3,2,1,0:T(8,128)(2,1)S(1)} %bitcast.4), custom_call_target="tpu_custom_call" | custom-call | flops 2000000000 | bytes 1000000 | tf_op jit(solution)/shard_map/pallas_call | solution.py:265
  15.5 0.0 copy-start.2
  15.5 0.0 collective-permute-done.7.rest_1_
  15.5 0.7 %shard_map.84.rest_2_ = f32[8,16,128]{2,1,0:T(8,128)S(1)} custom-call(s32[8,32]{1,0:T(8,128)S(1)} %bitcast.6, s32[1,32]{1,0:T(1,128)S(1)} %bitcast.9, bf16[32,16,128]{2,1,0:T(8,128)(2,1)S(1)} %get-tuple-element.14.density, bf16[16,16,128]{2,1,0:T(8,128)(2,1)S(1)} %collective-permute-done.6.rest_0_, bf16[16,16,128]{2,1,0:T(8,128)(2,1)S(1)} %collective-permute-done.7.rest_1_, ...), custom_call_target="tpu_custom_call" | custom-call | flops 2000000000 | bytes 1000000 | tf_op jit(solution)/shard_map/pallas_call | solution.py:265
  16.2 0.8 %shard_map.83.rest_1_ = f32[8,16,128]{2,1,0:T(8,128)S(1)} custom-call(s32[8,32]{1,0:T(8,128)S(1)} %bitcast.7, s32[1,32]{1,0:T(1,128)S(1)} %bitcast.10, bf16[32,16,128]{2,1,0:T(8,128)(2,1)S(1)} %get-tuple-element.14.density, bf16[16,16,128]{2,1,0:T(8,128)(2,1)S(1)} %collective-permute-done.6.rest_0_, bf16[16,16,128]{2,1,0:T(8,128)(2,1)S(1)} %collective-permute-done.7.rest_1_, ...), custom_call_target="tpu_custom_call" | custom-call | flops 2000000000 | bytes 1000000 | tf_op jit(solution)/shard_map/pallas_call | solution.py:265
  17.0 0.0 collective-permute-done.4.last
  17.0 0.0 copy-done.2
  17.0 1.0 %far.1 = bf16[32,16,128]{2,1,0:T(8,128)(2,1)} custom-call(f32[2,32,8,128]{3,2,1,0:T(8,128)S(1)} %get-tuple-element.11.weights, s32[32,8,128]{2,1,0:T(8,128)S(1)} %get-tuple-element.12.second, bf16[32,128,128]{2,1,0:T(8,128)(2,1)S(1)} %copy-done.2, f32[2,16,128]{2,1,0:T(8,128)S(1)} %partial.1.known, bf16[256,128]{1,0:T(8,128)(2,1)S(1)} %collective-permute-done.4.last, ...), custom_call_target="tpu_custom_call" | custom-call | flops 1000000000 | bytes 1000000 | tf_op jit(solution)/shard_map/far/pallas_call | solution.py:278
  (8 shorter events, 0.1 us)
Async XLA Ops:
  1.8 4.9 %collective-permute-start = (bf16[32,128]{1,0:T(8,128)(2,1)S(1)}, bf16[32,128]{1,0:T(8,128)(2,1)S(1)}, u32[]{:S(2)}, u32[]{:S(2)}) collective-permute-start(bf16[32,128]{1,0:T(8,128)(2,1)S(1)} %get-tuple-element.13.rest_0_), channel_id=1, source_target_pairs={{0,9},{1,8},{2,11},{3,10},{4,13},{5,12},{6,15},{7,14},{8,1},{9,0},... | collective-permute-start | bytes 24584 | tf_op jit(solution)/shard_map/ppermute | solution.py:168
  5.3 8.9 %collective-permute-start.5 = (bf16[16,16,128]{2,1,0:T(8,128)(2,1)S(1)}, bf16[16,16,128]{2,1,0:T(8,128)(2,1)S(1)}, u32[]{:S(2)}, u32[]{:S(2)}) collective-permute-start(bf16[16,16,128]{2,1,0:T(8,128)(2,1)S(1)} %get-tuple-element.15), channel_id=1, source_target_pairs={{0,1},{1,0},{2,3},{3,2},{4,5},{5,4},{6,7},{7,6},{8,9},{9,8},{10,11... | collective-permute-start | bytes 196616 | tf_op jit(solution)/shard_map/ppermute | solution.py:168
  6.0 8.2 %slice-start = ((s8[8388608]{0:T(1024)(128)(4,1)}), s8[4194304]{0:T(1024)(128)(4,1)S(1)}, s32[]{:S(2)}) async-start(s8[8388608]{0:T(1024)(128)(4,1)} %bitcast.3), calls=%async_computation | async-start | bytes 8388608
  6.0 3.5 %copy-start.3 = (f32[2,32]{1,0:T(2,128)S(1)}, f32[2,32]{1,0:T(2,128)}, u32[]{:S(2)}) copy-start(f32[2,32]{1,0:T(2,128)} %coupling.1) | copy-start | bytes 772
  6.0 3.5 %copy-start.4 = (s32[32]{0:T(128)S(1)}, s32[32]{0:T(128)}, u32[]{:S(2)}) copy-start(s32[32]{0:T(128)} %coarse_in.1) | copy-start | bytes 388
  6.0 8.2 %slice-start.1 = ((s8[8388608]{0:T(1024)(128)(4,1)}), s8[4194304]{0:T(1024)(128)(4,1)S(1)}, s32[]{:S(2)}) async-start(s8[8388608]{0:T(1024)(128)(4,1)} %bitcast.3), calls=%async_computation.1 | async-start | bytes 8388608
  6.0 8.2 %copy-start = (s32[32,8]{0,1:T(8,128)S(1)}, s32[32,8]{0,1:T(8,128)}, u32[]{:S(2)}) copy-start(s32[32,8]{0,1:T(8,128)} %param.10) | copy-start | bytes 3076
  6.0 8.2 %copy-start.1 = (s32[32]{0:T(128)S(1)}, s32[32]{0:T(128)}, u32[]{:S(2)}) copy-start(s32[32]{0:T(128)} %param.11) | copy-start | bytes 388
  6.0 8.1 %collective-permute-start.6 = (bf16[16,16,128]{2,1,0:T(8,128)(2,1)S(1)}, bf16[16,16,128]{2,1,0:T(8,128)(2,1)S(1)}, u32[]{:S(2)}, u32[]{:S(2)}) collective-permute-start(bf16[16,16,128]{2,1,0:T(8,128)(2,1)S(1)} %get-tuple-element.16), channel_id=1, source_target_pairs={{0,1},{1,2},{2,0},{3,4},{4,3},{5,6},{6,5},{7,8},{8,7},{9,10},{10,9... | collective-permute-start | bytes 196616 | tf_op jit(solution)/shard_map/ppermute | solution.py:222
  6.7 4.3 %collective-permute-start.1 = (bf16[64,128]{1,0:T(8,128)(2,1)S(1)}, bf16[64,128]{1,0:T(8,128)(2,1)S(1)}, u32[]{:S(2)}, u32[]{:S(2)}) collective-permute-start(bf16[64,128]{1,0:T(8,128)(2,1)S(1)} %get-tuple-element.18), channel_id=1, source_target_pairs={{0,7},{1,6},{2,5},{3,4},{4,3},{5,2},{6,1},{7,0},{8,15},{9,14},{10,... | collective-permute-start | bytes 49160 | tf_op jit(solution)/shard_map/ppermute | solution.py:168
  9.7 3.7 %collective-permute-start.3 = (bf16[64,128]{1,0:T(8,128)(2,1)S(1)}, bf16[64,128]{1,0:T(8,128)(2,1)S(1)}, u32[]{:S(2)}, u32[]{:S(2)}) collective-permute-start(bf16[64,128]{1,0:T(8,128)(2,1)S(1)} %get-tuple-element.18), channel_id=1, source_target_pairs={{0,3},{1,2},{2,1},{3,0},{4,7},{5,6},{6,5},{7,4},{8,11},{9,10},{10,... | collective-permute-start | bytes 49160 | tf_op jit(solution)/shard_map/ppermute | solution.py:168
  10.3 3.2 %collective-permute-start.2 = (bf16[64,128]{1,0:T(8,128)(2,1)S(1)}, bf16[64,128]{1,0:T(8,128)(2,1)S(1)}, u32[]{:S(2)}, u32[]{:S(2)}) collective-permute-start(bf16[64,128]{1,0:T(8,128)(2,1)S(1)} %get-tuple-element.18), channel_id=1, source_target_pairs={{0,5},{1,4},{2,7},{3,6},{4,1},{5,0},{6,3},{7,2},{8,13},{9,12},{10,... | collective-permute-start | bytes 49160 | tf_op jit(solution)/shard_map/ppermute | solution.py:168
  13.5 3.5 %collective-permute-start.4 = (bf16[256,128]{1,0:T(8,128)(2,1)S(1)}, bf16[256,128]{1,0:T(8,128)(2,1)S(1)}, u32[]{:S(2)}, u32[]{:S(2)}) collective-permute-start(bf16[256,128]{1,0:T(8,128)(2,1)S(1)} %constant_dynamic-update-slice_fusion.2), channel_id=1, source_target_pairs={{0,1},{1,0},{2,3},{3,2},{4,5},{5,4},{6,7},{7,6},{8,9},{9,8},{10,11... | collective-permute-start | bytes 196616 | tf_op jit(solution)/shard_map/ppermute | solution.py:168
  14.1 1.3 %collective-permute-start.7 = (bf16[16,16,128]{2,1,0:T(8,128)(2,1)S(1)}, bf16[16,16,128]{2,1,0:T(8,128)(2,1)S(1)}, u32[]{:S(2)}, u32[]{:S(2)}) collective-permute-start(bf16[16,16,128]{2,1,0:T(8,128)(2,1)S(1)} %collective-permute-done.6.rest_0_), channel_id=1, source_target_pairs={{0,1},{1,0},{2,3},{3,2},{4,5},{5,4},{6,7},{7,6},{8,9},{9,8},{10,11... | collective-permute-start | bytes 196616 | tf_op jit(solution)/shard_map/ppermute | solution.py:168
  15.5 1.5 %copy-start.2 = (bf16[32,128,128]{2,1,0:T(8,128)(2,1)S(1)}, bf16[32,128,128]{2,1,0:T(8,128)(2,1)}, u32[]{:S(2)}) copy-start(bf16[32,128,128]{2,1,0:T(8,128)(2,1)} %evaluate.1) | copy-start | bytes 3145732

commit v6 on v5

--- a/solution.py
+++ b/solution.py
@@ -121,13 +121,13 @@
         out[c] = coupled(pieces, weights, c, 0, out.shape[1])
 
 
-def far_kernel(cuts, weights, second, evaluate, known, last, *rest):
+def far_kernel(cuts, weights, second, evaluate, known, early, last, *rest):
     near, out = rest[:-1], rest[-1]
     blk_count, columns, panels = out.shape
     groups, slots = weights.shape[:2]
     local = []
     for c in range(groups):
-        total = known[c] + coupled((last,), weights, c, slots - last.shape[0] // columns, columns)
+        total = known[c] + coupled((early, last), weights, c, slots // 2, columns)
         local.append(total.astype(BF16))
     left = jnp.concatenate(local, axis=0)
     half = blk_count // 2
@@ -213,10 +213,14 @@
     )(*in_hbm(coarse_map, density, restrict))
 
     pieces = [moments]
-    for at, together in enumerate(rounds):
+    for at, together in enumerate(rounds[:-1]):
         sent = pieces[0] if at == 0 else jnp.concatenate(pieces, axis=0)
         for step in together:
             pieces.append(exchange(sent, step))
+    lasts = []
+    for part in (pieces[:-2], pieces[-2:]):
+        sent = jnp.concatenate(part, axis=0)
+        lasts.append(exchange(sent, 1))
 
     chip_halo = exchange(to_chip, 1)
     off_halo = lax.ppermute(to_off, "panel", off_pairs(count))
@@ -267,23 +271,23 @@
     make_partial = pl.pallas_call(
         partial_kernel,
         out_shape=pltpu.VMEM((groups, columns, panels), F32),
-        in_specs=[VMEM] * len(pieces),
+        in_specs=[VMEM] * (1 + len(pieces)),
         out_specs=VMEM,
         compiler_params=room(4),
         cost_estimate=cost(10**9, 10**6),
         name="partial",
     )
-    known = make_partial(*on_chip(weights, *pieces[:-1]))
+    known = make_partial(*on_chip(weights, *pieces))
 
     return pl.pallas_call(
         functools.partial(far_kernel, cuts),
         out_shape=jax.ShapeDtypeStruct(density.shape, BF16),
-        in_specs=[VMEM] * (5 + len(near)),
+        in_specs=[VMEM] * (6 + len(near)),
         out_specs=VMEM,
         compiler_params=room(4),
         cost_estimate=cost(10**9, 10**6),
         name="far",
-    )(*on_chip(weights, second, evaluate, known, pieces[-1], *near))
+    )(*on_chip(weights, second, evaluate, known, *lasts, *near))
 
 
 CUTS = ((True, 0, 8), (False, 0, 4), (False, 4, 8))

time: 18.1 us -> 18.9 us (1.044)
  waiting for transfers between devices: 3.15 us -> 4.02 us
    ppermute x7 -> x8, waiting for transfers between devices: 3.15 us -> 4.02 us  [exchange(): return lax.ppermute(x, 'panel', [(i, i ^ step) for i in range(count)])]
    ppermute x7 -> x8, starting transfers between devices: 8.91 us -> 8.91 us  [exchange(): return lax.ppermute(x, 'panel', [(i, i ^ step) for i in range(count)])]
  transfers between devices with their start and end apart: 8 -> 9, of which waited for: 3 -> 3; matrix products, arithmetic and copies ran while one was open for 0% -> 0% of each run, Pallas kernels for 16% -> 15%
where the time goes in v6:
time: 18.9 us; the launch traced here: 18.8 us
  starting transfers between devices  8.97 us (47%)
  Pallas kernels  5.62 us (30%)
  waiting for transfers between devices  4.02 us (21%)
    ppermute x8, starting transfers between devices, exchange(): return lax.ppermute(x, 'panel', [(i, i ^ step) for i in range(count)])  8.91 us
    ppermute x8, waiting for transfers between devices, exchange(): return lax.ppermute(x, 'panel', [(i, i ^ step) for i in range(count)])  4.02 us
    pallas_call x3, Pallas kernels, body(): near.append(call(*on_chip(ids, live_counts, kept, *halos, near_blocks)))  2.68 us
    pallas_call x1, Pallas kernels, body(): pl.pallas_call(functools.partial(moments_kernel, chunks), out_shape=(pltp...  1.76 us
    pallas_call x1, Pallas kernels, body(): pl.pallas_call(functools.partial(far_kernel, cuts), out_shape=jax.ShapeDt...  0.95 us
  transfers between devices with their start and end apart: 9, of which 3 were waited for; matrix products, arithmetic and copies ran while one was open for 0% of the time, Pallas kernels for 15%

profile of v6, /device:TPU:0, one launch (start us, length us, event | category | flops | bytes accessed | tf_op | source)
XLA Modules:
  0.0 18.8 jit_solution(1305355636356710502)
XLA Ops:
  0.0 1.8 %moments.1 = (bf16[32,128]{1,0:T(8,128)(2,1)S(1)}, bf16[32,16,128]{2,1,0:T(8,128)(2,1)S(1)}, bf16[16,16,128]{2,1,0:T(8,128)(2,1)S(1)}, bf16[16,16,128]{2,1,0:T(8,128)(2,1)S(1)}) custom-call(s32[32]{0:T(128)} %coarse_in.1, bf16[32,16,128]{2,1,0:T(8,128)(2,1)} %density_in.1, bf16[32,128,128]{2,1,0:T(8,128)(2,1)} %restrict_in.1), custom_call_target="tpu_custom_call" | custom-call | flops 10000000000 | bytes 1000000 | tf_op jit(solution)/shard_map/moments/pallas_call | solution.py:194
  1.8 3.6 %collective-permute-start = (bf16[32,128]{1,0:T(8,128)(2,1)S(1)}, bf16[32,128]{1,0:T(8,128)(2,1)S(1)}, u32[]{:S(2)}, u32[]{:S(2)}) collective-permute-start(bf16[32,128]{1,0:T(8,128)(2,1)S(1)} %get-tuple-element.13.rest_0_), channel_id=1, source_target_pairs={{0,9},{1,8},{2,11},{3,10},{4,13},{5,12},{6,15},{7,14},{8,1},{9,0},... | collective-permute-start | bytes 24584 | tf_op jit(solution)/shard_map/ppermute | solution.py:168
  5.3 0.7 %collective-permute-start.6 = (bf16[16,16,128]{2,1,0:T(8,128)(2,1)S(1)}, bf16[16,16,128]{2,1,0:T(8,128)(2,1)S(1)}, u32[]{:S(2)}, u32[]{:S(2)}) collective-permute-start(bf16[16,16,128]{2,1,0:T(8,128)(2,1)S(1)} %get-tuple-element.15), channel_id=1, source_target_pairs={{0,1},{1,0},{2,3},{3,2},{4,5},{5,4},{6,7},{7,6},{8,9},{9,8},{10,11... | collective-permute-start | bytes 196616 | tf_op jit(solution)/shard_map/ppermute | solution.py:168
  6.0 0.0 slice-start
  6.0 0.0 copy-start.3
  6.0 0.0 copy-start.4
  6.0 0.0 slice-start.1
  6.0 0.0 copy-start
  6.0 0.0 copy-start.1
  6.0 0.1 collective-permute-start.7
  6.1 0.6 %collective-permute-done.rest_1_ = bf16[32,128]{1,0:T(8,128)(2,1)S(1)} collective-permute-done((bf16[32,128]{1,0:T(8,128)(2,1)S(1)}, bf16[32,128]{1,0:T(8,128)(2,1)S(1)}, u32[]{:S(2)}, u32[]{:S(2)}) %collective-permute-start) | collective-permute-done | bytes 8224 | tf_op jit(solution)/shard_map/ppermute | solution.py:168
  6.7 2.2 %collective-permute-start.3 = (bf16[64,128]{1,0:T(8,128)(2,1)S(1)}, bf16[64,128]{1,0:T(8,128)(2,1)S(1)}, u32[]{:S(2)}, u32[]{:S(2)}) collective-permute-start(bf16[64,128]{1,0:T(8,128)(2,1)S(1)} %constant_dynamic-update-slice_fusion), channel_id=1, source_target_pairs={{0,3},{1,2},{2,1},{3,0},{4,7},{5,6},{6,5},{7,4},{8,11},{9,10},{10,... | collective-permute-start | bytes 49160 | tf_op jit(solution)/shard_map/ppermute | solution.py:168
  8.9 1.2 %collective-permute-start.2 = (bf16[64,128]{1,0:T(8,128)(2,1)S(1)}, bf16[64,128]{1,0:T(8,128)(2,1)S(1)}, u32[]{:S(2)}, u32[]{:S(2)}) collective-permute-start(bf16[64,128]{1,0:T(8,128)(2,1)S(1)} %constant_dynamic-update-slice_fusion), channel_id=1, source_target_pairs={{0,5},{1,4},{2,7},{3,6},{4,1},{5,0},{6,3},{7,2},{8,13},{9,12},{10,... | collective-permute-start | bytes 49160 | tf_op jit(solution)/shard_map/ppermute | solution.py:168
  10.1 0.0 copy-done.3
  10.1 0.0 copy-done.4
  10.1 0.2 %weights.1 = (f32[2,32,8,128]{3,2,1,0:T(8,128)S(1)}, s32[32,8,128]{2,1,0:T(8,128)S(1)}) custom-call(s32[1,32]{1,0:T(1,128)S(1)} %bitcast.11, f32[2,32]{1,0:T(2,128)S(1)} %copy-done.3, f32[8,128]{1,0:T(8,128)S(1)} %mark.1), custom_call_target="tpu_custom_call" | custom-call | flops 1000000000 | bytes 1000000 | tf_op jit(solution)/shard_map/weights/pallas_call | solution.py:250
  10.3 0.6 %collective-permute-start.1 = (bf16[64,128]{1,0:T(8,128)(2,1)S(1)}, bf16[64,128]{1,0:T(8,128)(2,1)S(1)}, u32[]{:S(2)}, u32[]{:S(2)}) collective-permute-start(bf16[64,128]{1,0:T(8,128)(2,1)S(1)} %constant_dynamic-update-slice_fusion), channel_id=1, source_target_pairs={{0,7},{1,6},{2,5},{3,4},{4,3},{5,2},{6,1},{7,0},{8,15},{9,14},{10,... | collective-permute-start | bytes 49160 | tf_op jit(solution)/shard_map/ppermute | solution.py:168
  10.9 0.0 collective-permute-done.3.rest_4_
  10.9 1.2 %collective-permute-done.2.rest_3_ = bf16[64,128]{1,0:T(8,128)(2,1)S(1)} collective-permute-done((bf16[64,128]{1,0:T(8,128)(2,1)S(1)}, bf16[64,128]{1,0:T(8,128)(2,1)S(1)}, u32[]{:S(2)}, u32[]{:S(2)}) %collective-permute-start.2) | collective-permute-done | bytes 16416 | tf_op jit(solution)/shard_map/ppermute | solution.py:168
  12.1 0.1 collective-permute-start.5
  12.2 2.2 %collective-permute-done.1.rest_2_ = bf16[64,128]{1,0:T(8,128)(2,1)S(1)} collective-permute-done((bf16[64,128]{1,0:T(8,128)(2,1)S(1)}, bf16[64,128]{1,0:T(8,128)(2,1)S(1)}, u32[]{:S(2)}, u32[]{:S(2)}) %collective-permute-start.1) | collective-permute-done | bytes 16416 | tf_op jit(solution)/shard_map/ppermute | solution.py:168
  14.4 0.1 collective-permute-start.4
  14.6 0.0 collective-permute-done.7.rest_0_
  14.6 0.5 %collective-permute-start.8 = (bf16[16,16,128]{2,1,0:T(8,128)(2,1)S(1)}, bf16[16,16,128]{2,1,0:T(8,128)(2,1)S(1)}, u32[]{:S(2)}, u32[]{:S(2)}) collective-permute-start(bf16[16,16,128]{2,1,0:T(8,128)(2,1)S(1)} %collective-permute-done.7.rest_0_), channel_id=1, source_target_pairs={{0,1},{1,0},{2,3},{3,2},{4,5},{5,4},{6,7},{7,6},{8,9},{9,8},{10,11... | collective-permute-start | bytes 196616 | tf_op jit(solution)/shard_map/ppermute | solution.py:168
  15.1 0.0 collective-permute-done.6.rest_0_
  15.1 0.0 slice-done
  15.1 0.0 slice-done.1
  15.1 0.0 copy-done
  15.1 0.0 copy-done.1
  15.1 1.2 %shard_map.82.rest_0_ = f32[16,16,128]{2,1,0:T(8,128)S(1)} custom-call(s32[8,32]{1,0:T(8,128)S(1)} %bitcast.5, s32[1,32]{1,0:T(1,128)S(1)} %bitcast.8, bf16[32,16,128]{2,1,0:T(8,128)(2,1)S(1)} %get-tuple-element.14.density, bf16[16,16,128]{2,1,0:T(8,128)(2,1)S(1)} %collective-permute-done.6.rest_0_, bf16[32,8,128,128]{3,2,1,0:T(8,128)(2,1)S(1)} %bitcast.4), custom_call_target="tpu_custom_call" | custom-call | flops 2000000000 | bytes 1000000 | tf_op jit(solution)/shard_map/pallas_call | solution.py:269
  16.3 0.0 copy-start.2
  16.3 0.0 collective-permute-done.8.rest_1_
  16.3 0.7 %shard_map.84.rest_2_ = f32[8,16,128]{2,1,0:T(8,128)S(1)} custom-call(s32[8,32]{1,0:T(8,128)S(1)} %bitcast.6, s32[1,32]{1,0:T(1,128)S(1)} %bitcast.9, bf16[32,16,128]{2,1,0:T(8,128)(2,1)S(1)} %get-tuple-element.14.density, bf16[16,16,128]{2,1,0:T(8,128)(2,1)S(1)} %collective-permute-done.7.rest_0_, bf16[16,16,128]{2,1,0:T(8,128)(2,1)S(1)} %collective-permute-done.8.rest_1_, ...), custom_call_target="tpu_custom_call" | custom-call | flops 2000000000 | bytes 1000000 | tf_op jit(solution)/shard_map/pallas_call | solution.py:269
  17.0 0.8 %shard_map.83.rest_1_ = f32[8,16,128]{2,1,0:T(8,128)S(1)} custom-call(s32[8,32]{1,0:T(8,128)S(1)} %bitcast.7, s32[1,32]{1,0:T(1,128)S(1)} %bitcast.10, bf16[32,16,128]{2,1,0:T(8,128)(2,1)S(1)} %get-tuple-element.14.density, bf16[16,16,128]{2,1,0:T(8,128)(2,1)S(1)} %collective-permute-done.7.rest_0_, bf16[16,16,128]{2,1,0:T(8,128)(2,1)S(1)} %collective-permute-done.8.rest_1_, ...), custom_call_target="tpu_custom_call" | custom-call | flops 2000000000 | bytes 1000000 | tf_op jit(solution)/shard_map/pallas_call | solution.py:269
  17.8 0.0 collective-permute-done.5.last
  17.8 0.0 collective-permute-done.4.early
  17.8 0.0 copy-done.2
  17.8 0.9 %far.1 = bf16[32,16,128]{2,1,0:T(8,128)(2,1)} custom-call(f32[2,32,8,128]{3,2,1,0:T(8,128)S(1)} %get-tuple-element.11.weights, s32[32,8,128]{2,1,0:T(8,128)S(1)} %get-tuple-element.12.second, bf16[32,128,128]{2,1,0:T(8,128)(2,1)S(1)} %copy-done.2, f32[2,16,128]{2,1,0:T(8,128)S(1)} %partial.1.known, bf16[128,128]{1,0:T(8,128)(2,1)S(1)} %collective-permute-done.4.early, ...), custom_call_target="tpu_custom_call" | custom-call | flops 1000000000 | bytes 1000000 | tf_op jit(solution)/shard_map/far/pallas_call | solution.py:282
  (7 shorter events, 0.1 us)
Async XLA Ops:
  1.8 4.9 %collective-permute-start = (bf16[32,128]{1,0:T(8,128)(2,1)S(1)}, bf16[32,128]{1,0:T(8,128)(2,1)S(1)}, u32[]{:S(2)}, u32[]{:S(2)}) collective-permute-start(bf16[32,128]{1,0:T(8,128)(2,1)S(1)} %get-tuple-element.13.rest_0_), channel_id=1, source_target_pairs={{0,9},{1,8},{2,11},{3,10},{4,13},{5,12},{6,15},{7,14},{8,1},{9,0},... | collective-permute-start | bytes 24584 | tf_op jit(solution)/shard_map/ppermute | solution.py:168
  5.3 9.7 %collective-permute-start.6 = (bf16[16,16,128]{2,1,0:T(8,128)(2,1)S(1)}, bf16[16,16,128]{2,1,0:T(8,128)(2,1)S(1)}, u32[]{:S(2)}, u32[]{:S(2)}) collective-permute-start(bf16[16,16,128]{2,1,0:T(8,128)(2,1)S(1)} %get-tuple-element.15), channel_id=1, source_target_pairs={{0,1},{1,0},{2,3},{3,2},{4,5},{5,4},{6,7},{7,6},{8,9},{9,8},{10,11... | collective-permute-start | bytes 196616 | tf_op jit(solution)/shard_map/ppermute | solution.py:168
  6.0 9.0 %slice-start = ((s8[8388608]{0:T(1024)(128)(4,1)}), s8[4194304]{0:T(1024)(128)(4,1)S(1)}, s32[]{:S(2)}) async-start(s8[8388608]{0:T(1024)(128)(4,1)} %bitcast.3), calls=%async_computation | async-start | bytes 8388608
  6.0 4.1 %copy-start.3 = (f32[2,32]{1,0:T(2,128)S(1)}, f32[2,32]{1,0:T(2,128)}, u32[]{:S(2)}) copy-start(f32[2,32]{1,0:T(2,128)} %coupling.1) | copy-start | bytes 772
  6.0 4.1 %copy-start.4 = (s32[32]{0:T(128)S(1)}, s32[32]{0:T(128)}, u32[]{:S(2)}) copy-start(s32[32]{0:T(128)} %coarse_in.1) | copy-start | bytes 388
  6.0 9.0 %slice-start.1 = ((s8[8388608]{0:T(1024)(128)(4,1)}), s8[4194304]{0:T(1024)(128)(4,1)S(1)}, s32[]{:S(2)}) async-start(s8[8388608]{0:T(1024)(128)(4,1)} %bitcast.3), calls=%async_computation.1 | async-start | bytes 8388608
  6.0 9.0 %copy-start = (s32[32,8]{0,1:T(8,128)S(1)}, s32[32,8]{0,1:T(8,128)}, u32[]{:S(2)}) copy-start(s32[32,8]{0,1:T(8,128)} %param.10) | copy-start | bytes 3076
  6.0 9.0 %copy-start.1 = (s32[32]{0:T(128)S(1)}, s32[32]{0:T(128)}, u32[]{:S(2)}) copy-start(s32[32]{0:T(128)} %param.11) | copy-start | bytes 388
  6.0 8.5 %collective-permute-start.7 = (bf16[16,16,128]{2,1,0:T(8,128)(2,1)S(1)}, bf16[16,16,128]{2,1,0:T(8,128)(2,1)S(1)}, u32[]{:S(2)}, u32[]{:S(2)}) collective-permute-start(bf16[16,16,128]{2,1,0:T(8,128)(2,1)S(1)} %get-tuple-element.16), channel_id=1, source_target_pairs={{0,1},{1,2},{2,0},{3,4},{4,3},{5,6},{6,5},{7,8},{8,7},{9,10},{10,9... | collective-permute-start | bytes 196616 | tf_op jit(solution)/shard_map/ppermute | solution.py:226
  6.7 4.2 %collective-permute-start.3 = (bf16[64,128]{1,0:T(8,128)(2,1)S(1)}, bf16[64,128]{1,0:T(8,128)(2,1)S(1)}, u32[]{:S(2)}, u32[]{:S(2)}) collective-permute-start(bf16[64,128]{1,0:T(8,128)(2,1)S(1)} %constant_dynamic-update-slice_fusion), channel_id=1, source_target_pairs={{0,3},{1,2},{2,1},{3,0},{4,7},{5,6},{6,5},{7,4},{8,11},{9,10},{10,... | collective-permute-start | bytes 49160 | tf_op jit(solution)/shard_map/ppermute | solution.py:168
  8.9 3.2 %collective-permute-start.2 = (bf16[64,128]{1,0:T(8,128)(2,1)S(1)}, bf16[64,128]{1,0:T(8,128)(2,1)S(1)}, u32[]{:S(2)}, u32[]{:S(2)}) collective-permute-start(bf16[64,128]{1,0:T(8,128)(2,1)S(1)} %constant_dynamic-update-slice_fusion), channel_id=1, source_target_pairs={{0,5},{1,4},{2,7},{3,6},{4,1},{5,0},{6,3},{7,2},{8,13},{9,12},{10,... | collective-permute-start | bytes 49160 | tf_op jit(solution)/shard_map/ppermute | solution.py:168
  10.3 4.1 %collective-permute-start.1 = (bf16[64,128]{1,0:T(8,128)(2,1)S(1)}, bf16[64,128]{1,0:T(8,128)(2,1)S(1)}, u32[]{:S(2)}, u32[]{:S(2)}) collective-permute-start(bf16[64,128]{1,0:T(8,128)(2,1)S(1)} %constant_dynamic-update-slice_fusion), channel_id=1, source_target_pairs={{0,7},{1,6},{2,5},{3,4},{4,3},{5,2},{6,1},{7,0},{8,15},{9,14},{10,... | collective-permute-start | bytes 49160 | tf_op jit(solution)/shard_map/ppermute | solution.py:168
  12.1 5.7 %collective-permute-start.5 = (bf16[128,128]{1,0:T(8,128)(2,1)S(1)}, bf16[128,128]{1,0:T(8,128)(2,1)S(1)}, u32[]{:S(2)}, u32[]{:S(2)}) collective-permute-start(bf16[128,128]{1,0:T(8,128)(2,1)S(1)} %pad_maximum_fusion.1), channel_id=1, source_target_pairs={{0,1},{1,0},{2,3},{3,2},{4,5},{5,4},{6,7},{7,6},{8,9},{9,8},{10,11... | collective-permute-start | bytes 98312 | tf_op jit(solution)/shard_map/ppermute | solution.py:168
  14.4 3.4 %collective-permute-start.4 = (bf16[128,128]{1,0:T(8,128)(2,1)S(1)}, bf16[128,128]{1,0:T(8,128)(2,1)S(1)}, u32[]{:S(2)}, u32[]{:S(2)}) collective-permute-start(bf16[128,128]{1,0:T(8,128)(2,1)S(1)} %pad_maximum_fusion), channel_id=1, source_target_pairs={{0,1},{1,0},{2,3},{3,2},{4,5},{5,4},{6,7},{7,6},{8,9},{9,8},{10,11... | collective-permute-start | bytes 98312 | tf_op jit(solution)/shard_map/ppermute | solution.py:168
  14.6 1.7 %collective-permute-start.8 = (bf16[16,16,128]{2,1,0:T(8,128)(2,1)S(1)}, bf16[16,16,128]{2,1,0:T(8,128)(2,1)S(1)}, u32[]{:S(2)}, u32[]{:S(2)}) collective-permute-start(bf16[16,16,128]{2,1,0:T(8,128)(2,1)S(1)} %collective-permute-done.7.rest_0_), channel_id=1, source_target_pairs={{0,1},{1,0},{2,3},{3,2},{4,5},{5,4},{6,7},{7,6},{8,9},{9,8},{10,11... | collective-permute-start | bytes 196616 | tf_op jit(solution)/shard_map/ppermute | solution.py:168
  16.3 1.5 %copy-start.2 = (bf16[32,128,128]{2,1,0:T(8,128)(2,1)S(1)}, bf16[32,128,128]{2,1,0:T(8,128)(2,1)}, u32[]{:S(2)}) copy-start(bf16[32,128,128]{2,1,0:T(8,128)(2,1)} %evaluate.1) | copy-start | bytes 3145732
